TPU v7x, 32 devices: a 4x2x2 block of a 4x4x8 slice. The times are simulated.
32 devices in a mesh: batch: 4 (over y, z), dap: 8 (over x, core).
Axes of the slice: x: 4, y: 2, z: 2, core: 2. Of those that a mesh axis runs over, the one named last changes fastest.
The devices are a block of a 4x4x8 slice.
Arguments:
- z_pair: bfloat16 [1024, 256, 128], P(('batch', 'dap')), parts along dimension 0
- msa_feat: bfloat16 [512, 1024, 64], P(None, ('batch', 'dap')), parts along dimension 1
- ln_scale: bfloat16 [64], replicated
- ln_offset: bfloat16 [64], replicated
- w_a: bfloat16 [64, 32], replicated
- b_a: bfloat16 [32], replicated
- w_b: bfloat16 [64, 32], replicated
- b_b: bfloat16 [32], replicated
- w_out: bfloat16 [1024, 128], replicated
- b_out: bfloat16 [128], replicated
Outputs:
- output: bfloat16 [1024, 256, 128], P(('batch', 'dap')), parts along dimension 0
There are 4 independent parts. A program takes and returns all parts, laid end to end along the dimension named above; an argument that names none is the same for every part.
All inputs are finite; a program needn't handle non-finite values.
Results may differ from a plain program's by a relative error of at most 0.001.
Values are sent between devices in bfloat16 or wider.
A program may use at most 768 MiB of HBM per device.

v0:
```python
import jax
import jax.numpy as jnp
from jax import lax
from jax.sharding import PartitionSpec as P

LN_EPS = 1e-5
ROW_BUDGET = 8192


def layer_norm(array_b8, ln_scale, ln_offset):
    value_a7 = array_b8.astype(jnp.float32)
    mean_val = jnp.mean(value_a7, axis=-1, keepdims=True)
    centred = value_a7 - mean_val
    var_val = jnp.mean(centred * centred, axis=-1, keepdims=True)
    normed = centred * lax.rsqrt(var_val + LN_EPS)
    return (normed * ln_scale.astype(jnp.float32) + ln_offset.astype(jnp.float32)).astype(jnp.bfloat16)


def project(local_c8, weight, bias_vec):
    out_f32 = jnp.einsum('snm,mc->snc', local_c8, weight, preferred_element_type=jnp.float32)
    return (out_f32 + bias_vec.astype(jnp.float32)).astype(jnp.bfloat16)


def outer_update(z_rows, proj_a, full_b, w_out, b_out):
    n_seq, n_loc, hid_dim = proj_a.shape
    n_res = full_b.shape[1]
    pair_dim = z_rows.shape[2]
    row_tile = min(n_loc, max(1, ROW_BUDGET // n_res))
    w_cube = w_out.reshape(hid_dim, hid_dim, pair_dim)
    bias_out = b_out.astype(jnp.float32)
    inv_seq = 1.0 / n_seq

    def tile_body(tile_idx, z_acc):
        row_start = tile_idx * row_tile
        a_tile = lax.dynamic_slice_in_dim(proj_a, row_start, row_tile, axis=1)
        z_tile = lax.dynamic_slice_in_dim(z_acc, row_start, row_tile, axis=0)
        outer_prod = jnp.einsum('sic,sjd->icjd', a_tile, full_b, preferred_element_type=jnp.float32)
        outer_prod = (outer_prod * inv_seq).astype(jnp.bfloat16)
        update = jnp.einsum('icjd,cdz->ijz', outer_prod, w_cube, preferred_element_type=jnp.float32) + bias_out
        new_tile = (z_tile.astype(jnp.float32) + update).astype(jnp.bfloat16)
        return lax.dynamic_update_slice_in_dim(z_acc, new_tile, row_start, axis=0)

    return lax.fori_loop(0, n_loc // row_tile, tile_body, z_rows)


def solution(mesh):
    row_spec = P(('batch', 'dap'))
    col_spec = P(None, ('batch', 'dap'))
    rep_spec = P()

    def local_update(z_rows, value_a8, ln_scale, ln_offset, w_a, b_a, w_b, b_b, w_out, b_out):
        local_c8 = layer_norm(value_a8, ln_scale, ln_offset)
        proj_a = project(local_c8, w_a, b_a)
        proj_b = project(local_c8, w_b, b_b)
        full_b = lax.all_gather(proj_b, 'dap', axis=1, tiled=True)
        return outer_update(z_rows, proj_a, full_b, w_out, b_out)

    return jax.shard_map(local_update, mesh=mesh, in_specs=(row_spec, col_spec) + (rep_spec,) * 8, out_specs=row_spec, check_vma=False)
```

profile of v0, /device:TPU:81, one launch (start us, length us, event | category | flops | bytes accessed | tf_op | source)
XLA Modules:
  0.0 98.3 jit_solution(12914613836155641692)
XLA Ops:
  6.5 0.0 copy-start
  6.6 0.0 copy-start.1
  6.6 0.0 all-gather.2.cloned.1.call-start
  6.6 0.8 convert_element_type.41
  7.4 0.7 convert_element_type.42
  8.0 0.7 convert_element_type.46
  8.7 0.0 copy-start.3
  8.7 2.0 %convert_reduce_fusion = f32[512,32]{0,1:T(8,128)S(1)} fusion(bf16[512,32,64]{0,2,1:T(8,128)(2,1)} %param.11), kind=kLoop, calls=%fused_computation.7 | loop fusion | flops 2080768 | bytes 2162688 | tf_op jit(solution)/shard_map/reduce_sum | solution.py:12
  10.7 2.3 %fusion.10 = f32[512,32]{0,1:T(8,128)S(1)} fusion(bf16[512,32,64]{0,2,1:T(8,128)(2,1)} %param.11, f32[512,32]{0,1:T(8,128)S(1)} %broadcast_multiply_fusion), kind=kLoop, calls=%fused_computation.10 | loop fusion | flops 4177920 | bytes 2228224 | tf_op jit(solution)/shard_map/reduce_sum | solution.py:14
  13.1 0.0 copy-done.1
  13.1 0.0 copy-start.5
  13.1 0.0 copy-start.6
  13.1 0.0 copy-start.4
  13.1 0.9 fusion.13
  14.1 0.0 copy-start.2
  14.1 1.3 %copy-done.2 = bf16[512,32,64]{0,2,1:T(8,128)(2,1)} copy-done((bf16[512,32,64]{0,2,1:T(8,128)(2,1)}, bf16[512,32,64]{0,2,1:T(8,128)(2,1)S(1)}, u32[]{:S(2)}) %copy-start.2) | copy-done | bytes 2097176
  15.4 0.0 copy-done.3
  15.4 1.5 %add_convert_fusion = bf16[512,32,32]{0,2,1:T(8,128)(2,1)} fusion(bf16[512,32,64]{0,2,1:T(8,128)(2,1)S(1)} %fusion.13, f32[32]{0:T(128)S(1)} %convert_element_type.46, bf16[64,32]{0,1:T(8,128)(2,1)S(1)} %copy-done.3), kind=kOutput, calls=%fused_computation.17 | convolution fusion | flops 68157440 | bytes 3149952 | tf_op jit(solution)/shard_map/snm,mc->snc/dot_general | solution.py:20
  16.9 0.1 all-gather.2.cloned.1.call-update
  16.9 0.0 copy-done.5
  17.0 0.0 copy-done.6
  17.0 0.0 copy-done.4
  17.0 2.0 %fusion.18 = bf16[512,32,32,1]{0,2,3,1:T(8,128)(2,1)S(1)} fusion(bf16[512,32,64]{0,2,1:T(8,128)(2,1)} %copy-done.2, f32[32]{0:T(128)S(1)} %convert_element_type.44, bf16[64,32]{0,1:T(8,128)(2,1)S(1)} %copy-done.4), kind=kOutput, calls=%fused_computation.19 | convolution fusion | flops 68157440 | bytes 3149952 | tf_op jit(solution)/shard_map/snm,mc->snc/dot_general | solution.py:20
  19.0 49.0 %all-gather.2.cloned.1.call-done = bf16[512,256,32]{0,2,1:T(8,128)(2,1)} async-done(((bf16[512,32,32]{0,2,1:T(8,128)(2,1)}), bf16[512,256,32]{0,2,1:T(8,128)(2,1)}) %all-gather.2.cloned.1.call-update) | async-done | bytes 8388624 | tf_op jit(solution)/shard_map/all_gather | solution.py:55
  68.0 0.0 copy-done
  68.0 23.4 %fusion.15 = bf16[32,256,128]{2,1,0:T(8,128)(2,1)} fusion(bf16[32,256,128]{2,1,0:T(8,128)(2,1)} %param.10, bf16[512,32,32,1]{0,2,3,1:T(8,128)(2,1)S(1)} %fusion.18, bf16[512,256,32]{0,2,1:T(8,128)(2,1)} %all-gather.2.cloned.1.call-done, f32[128]{0:T(128)S(1)} %convert_element_type.49, bf16[32,32,128,1]{2,1,0,3:T(8,128)(2,1)S(1)} %bitcast.29), kind=kOutput, calls=%fused_computation.16 | convolution fusion | flops 10758389760 | bytes 13894144 | tf_op jit(solution)/shard_map/while/body/eval_jaxpr/icjd,cdz->ijz/dot_general | solution.py:39
  (4 shorter events, 0.0 us)
Async XLA Ops:
  6.5 61.5 %copy-start = (bf16[1024,128]{1,0:T(8,128)(2,1)S(1)}, bf16[1024,128]{1,0:T(8,128)(2,1)}, u32[]{:S(2)}) copy-start(bf16[1024,128]{1,0:T(8,128)(2,1)} %param.18) | copy-start | bytes 786436
  6.6 6.5 %copy-start.1 = (bf16[512,32,64]{0,2,1:T(8,128)(2,1)S(1)}, bf16[512,32,64]{0,2,1:T(8,128)(2,1)}, u32[]{:S(2)}) copy-start(bf16[512,32,64]{0,2,1:T(8,128)(2,1)} %param.11) | copy-start | bytes 6291460
  6.6 61.5 %all-gather.2.cloned.1.call-start = ((), (), s32[]{:S(2)}) async-start(), calls=%async_computation | async-start | bytes 9437184 | tf_op jit(solution)/shard_map/all_gather | solution.py:55
  8.7 6.7 %copy-start.3 = (bf16[64,32]{0,1:T(8,128)(2,1)S(1)}, bf16[64,32]{0,1:T(8,128)(2,1)}, u32[]{:S(2)}) copy-start(bf16[64,32]{0,1:T(8,128)(2,1)} %param.16) | copy-start | bytes 12292
  13.1 3.8 %copy-start.5 = (bf16[32]{0:T(256)(128)(2,1)S(1)}, bf16[32]{0:T(256)(128)(2,1)}, u32[]{:S(2)}) copy-start(bf16[32]{0:T(256)(128)(2,1)} %param.15) | copy-start | bytes 196
  13.1 3.9 %copy-start.6 = (bf16[128]{0:T(256)(128)(2,1)S(1)}, bf16[128]{0:T(256)(128)(2,1)}, u32[]{:S(2)}) copy-start(bf16[128]{0:T(256)(128)(2,1)} %param.19) | copy-start | bytes 772
  13.1 3.9 %copy-start.4 = (bf16[64,32]{0,1:T(8,128)(2,1)S(1)}, bf16[64,32]{0,1:T(8,128)(2,1)}, u32[]{:S(2)}) copy-start(bf16[64,32]{0,1:T(8,128)(2,1)} %param.14) | copy-start | bytes 12292
  14.1 1.3 %copy-start.2 = (bf16[512,32,64]{0,2,1:T(8,128)(2,1)}, bf16[512,32,64]{0,2,1:T(8,128)(2,1)S(1)}, u32[]{:S(2)}) copy-start(bf16[512,32,64]{0,2,1:T(8,128)(2,1)S(1)} %fusion.13) | copy-start | bytes 6291460
Sparse Core Ops, SparseCore 0:
  17.1 50.9 all-gather.1
where the time goes:
time: 98.5 us; the launch traced here: 98.3 us
  waiting for transfers between devices  49.1 us (50%)
  matrix products  26.9 us (27%)
  between operations  13.5 us (14%)
  other arithmetic  7.44 us (8%)
  local copies, waits for them, and re-layouts  1.34 us (1%)
    all_gather x1, waiting for transfers between devices, local_update(): full_b = lax.all_gather(proj_b, 'dap', axis=1, tiled=True)  49 us
    dot_general x1, matrix products, tile_body(): jnp.einsum('icjd,cdz->ijz', outer_prod, w_cube, preferred_element_type=jn...  23.4 us
    dot_general x2, matrix products, project(): jnp.einsum('snm,mc->snc', local_c8, weight, preferred_element_type=jnp.fl...  3.5 us
    reduce_sum x1, other arithmetic, layer_norm(): var_val = jnp.mean(centred * centred, axis=-1, keepdims=True)  2.32 us
    reduce_sum x1, other arithmetic, layer_norm(): mean_val = jnp.mean(value_a7, axis=-1, keepdims=True)  2.02 us
  transfers between devices with their start and end apart: 1, of which 1 were waited for; matrix products, arithmetic and copies ran while one was open for 2% of the time, Pallas kernels for 0%

commit v1 on v0

v1 whole, which is shorter than its diff:
```python
import functools

import jax
import jax.numpy as jnp
from jax import lax
from jax.experimental import pallas as pl
from jax.experimental.pallas import tpu as pltpu
from jax.sharding import PartitionSpec as P

LN_EPS = 1e-5
F32 = jnp.float32
BF16 = jnp.bfloat16
LANES = 128
HALF = 16
PIECES = 4
MESH = pl.DeviceIdType.MESH


def iota(shape, dim):
    return lax.broadcasted_iota(jnp.int32, shape, dim)


def column_lanes(row, count):
    spread = jnp.broadcast_to(row, (count, count))
    picked = jnp.where(iota((count, count), 0) == iota((count, count), 1), spread, 0.0)
    return jnp.broadcast_to(jnp.sum(picked, axis=1, keepdims=True), (count, LANES))


def kernel(n_dev, z_hbm, x_hbm, ls_hbm, lo_hbm, wa_hbm, ba_hbm, wb_hbm, bb_hbm, wo_hbm, bo_hbm, out_hbm,
           z_buf, x_buf, ls_v, lo_v, wa_v, ba_v, wb_v, bb_v, wo_v, bo_v,
           scale_bc, offset_bc, bias_a, bias_b, row_bc, proj_a_w, proj_b_w, a_mat, bt, o_mat, w_f32, w_diag, u_acc,
           small_sem, x_sem, z_sem, out_sem, recv_sem, right_sem, left_sem, sib_sem):
    n_seq = x_hbm.shape[1]
    n_loc = z_hbm.shape[0]
    m_dim = wa_hbm.shape[1]
    hid = wa_hbm.shape[0]
    inv_seq = 1.0 / n_seq
    me = lax.axis_index('dap')
    core = lax.rem(me, 2)
    sib = me + 1 - 2 * core
    right = lax.rem(me + 2, n_dev)
    left = lax.rem(me + n_dev - 2, n_dev)

    barrier = pltpu.get_barrier_semaphore()
    for peer in (sib, right, left):
        pl.semaphore_signal(barrier, inc=1, device_id={'dap': peer}, device_id_type=MESH)

    small = [pltpu.make_async_copy(src, dst, small_sem.at[k]) for k, (src, dst) in enumerate((
        (wb_hbm, wb_v), (bb_hbm, bb_v), (ls_hbm, ls_v), (lo_hbm, lo_v), (wa_hbm, wa_v), (ba_hbm, ba_v),
        (wo_hbm, wo_v), (bo_hbm, bo_v)))]
    x_rows = 4 * m_dim
    x_copies = [pltpu.make_async_copy(x_hbm.at[pl.ds(k * x_rows, x_rows)], x_buf.at[pl.ds(k * x_rows, x_rows)], x_sem.at[k])
                for k in range(n_loc // 4)]
    for copy in small[:4]:
        copy.start()
    for copy in x_copies[:4]:
        copy.start()
    for copy in small[4:6]:
        copy.start()
    for copy in x_copies[4:]:
        copy.start()
    for copy in small[6:]:
        copy.start()
    z_copy = pltpu.make_async_copy(z_hbm, z_buf, z_sem)
    z_copy.start()

    for copy in small[:4]:
        copy.wait()
    row_bc[...] = column_lanes(bb_v[...].astype(F32).reshape(1, hid), hid)
    wb_rows = wb_v[...].astype(F32)
    wb_two = jnp.concatenate([wb_rows, wb_rows], axis=1)
    scale_bc[...] = column_lanes(ls_v[...].astype(F32).reshape(1, m_dim), m_dim)
    offset_bc[...] = column_lanes(lo_v[...].astype(F32).reshape(1, m_dim), m_dim)
    in_half = iota((HALF, LANES), 0)
    in_pair = iota((HALF, LANES), 1) // m_dim
    for d in range(hid):
        spread = jnp.broadcast_to(wb_two[d:d + 1, :], (HALF, LANES))
        for t in range(HALF * m_dim // LANES):
            part = jnp.where(in_half == in_pair + 2 * t, spread, 0.0)
            proj_b_w[d * HALF:(d + 1) * HALF, t * LANES:(t + 1) * LANES] = part.astype(BF16)
        bias_b[d * HALF:(d + 1) * HALF, :] = jnp.broadcast_to(row_bc[d:d + 1, :], (HALF, LANES))

    def norm_residue(n):
        rows = pl.ds(pl.multiple_of(n * m_dim, m_dim), m_dim)
        value = x_buf[rows, :].astype(F32)
        mean = jnp.sum(value, axis=0, keepdims=True) * (1.0 / m_dim)
        centred = value - mean
        var = jnp.sum(centred * centred, axis=0, keepdims=True) * (1.0 / m_dim)
        normed = centred * lax.rsqrt(var + LN_EPS)
        lanes4 = n_seq // LANES
        scale = jnp.concatenate([scale_bc[...]] * lanes4, axis=1)
        offset = jnp.concatenate([offset_bc[...]] * lanes4, axis=1)
        x_buf[rows, :] = (normed * scale + offset).astype(BF16)

    rows_piece = HALF * hid // PIECES

    def remote(src, dst, send, recv, peer):
        return pltpu.make_async_remote_copy(src_ref=src, dst_ref=dst, send_sem=send, recv_sem=recv,
                                            device_id={'dap': peer}, device_id_type=MESH)

    def slot_of(q, r, h):
        return q * 8 + r * 2 + h

    def to_right(r, h, c):
        r_there = (r + 3) % 4
        k = (0 if r == 0 else 2) + (h if r == 0 else 0)
        return remote(bt.at[slot_of(0, r, h), c], bt.at[slot_of(0, r_there, h), c], right_sem.at[k, c],
                      recv_sem.at[slot_of(0, r_there, h), c], right)

    def to_left(r, h, c):
        r_there = (r + 1) % 4
        k = (0 if r == 0 else 2) + (h if r == 0 else 0)
        return remote(bt.at[slot_of(0, r, h), c], bt.at[slot_of(0, r_there, h), c], left_sem.at[k, c],
                      recv_sem.at[slot_of(0, r_there, h), c], left)

    def to_sib(r, h, c):
        return remote(bt.at[slot_of(0, r, h), c], bt.at[slot_of(1, r, h), c], sib_sem.at[r * 2 + h, c],
                      recv_sem.at[slot_of(1, r, h), c], sib)

    def arrived(slot, c):
        remote(bt.at[slot, c], bt.at[slot, c], sib_sem.at[0, 0], recv_sem.at[slot, c], sib).wait_recv()

    sent = []

    def send(copy):
        copy.start()
        sent.append(copy)

    bias_four = None
    for h in range(2):
        for k in range(4):
            x_copies[h * 4 + k].wait()

            def body(n, carry):
                norm_residue(n)
                return carry

            lax.fori_loop((h * 4 + k) * 4, (h * 4 + k + 1) * 4, body, 0, unroll=2)
        normed = x_buf.at[pl.ds(h * HALF * m_dim, HALF * m_dim), :]
        for c in range(PIECES):
            rows = slice(c * rows_piece, (c + 1) * rows_piece)
            res = jnp.dot(proj_b_w[rows, :], normed[...], preferred_element_type=F32)
            bias = jnp.concatenate([bias_b[rows, :]] * (n_seq // LANES), axis=1)
            bt[slot_of(0, 0, h), c] = (res + bias).astype(BF16)
        if h == 0:
            pl.semaphore_wait(barrier, 3)
        for c in range(PIECES):
            send(to_right(0, h, c))
            send(to_left(0, h, c))
            send(to_sib(0, h, c))

    for copy in small[4:]:
        copy.wait()
    row_bc[...] = column_lanes(ba_v[...].astype(F32).reshape(1, hid), hid)
    bias_a[...] = jnp.concatenate([row_bc[...]] * 4, axis=0)
    wa_rows = wa_v[...].astype(F32)
    wa_wide = jnp.concatenate([jnp.concatenate([wa_rows] * 4, axis=1)] * 4, axis=0)
    same = (iota(wa_wide.shape, 0) // hid) == (iota(wa_wide.shape, 1) // m_dim)
    proj_a_w[...] = jnp.where(same, wa_wide, 0.0).astype(BF16)
    for g in range(n_loc // 4):
        res = jnp.dot(proj_a_w[...], x_buf[g * x_rows:(g + 1) * x_rows, :], preferred_element_type=F32)
        res = res + jnp.concatenate([bias_a[...]] * (n_seq // LANES), axis=1)
        a_mat[:, g * LANES:(g + 1) * LANES] = res.T.astype(BF16)

    w_f32[...] = wo_v[...].astype(F32)
    w_diag[...] = jnp.zeros_like(w_diag)

    def spread_w(d, carry):
        block = w_f32[pl.ds(d, hid, stride=hid), :].astype(BF16)
        c = d // 8
        for k in range(4):
            row = pl.multiple_of((d - c * 8) * LANES + k * hid, hid)
            w_diag[c, pl.ds(row, hid), k * LANES:(k + 1) * LANES] = block
        return carry

    lax.fori_loop(0, hid, spread_w, 0)

    def outer_piece(slot, c):
        res = jnp.dot(bt[slot, c], a_mat[...], preferred_element_type=F32)
        res = (res * inv_seq).astype(BF16)
        for d in range(8):
            for g in range(8):
                o_mat[c, g * HALF:(g + 1) * HALF, d * LANES:(d + 1) * LANES] = (
                    res[d * HALF:(d + 1) * HALF, g * LANES:(g + 1) * LANES])

    def project_piece(c):
        return jnp.dot(o_mat[c], w_diag[c], preferred_element_type=F32)

    chip = me // 2

    def column_of(q, r, h):
        src = lax.rem(chip + r, n_dev // 2) * 2 + (core if q == 0 else 1 - core)
        return pl.multiple_of(src * (2 * HALF) + h * HALF, HALF)

    def out_copy(q, r, h):
        cols = pl.ds(column_of(q, r, h), HALF)
        return pltpu.make_async_copy(z_buf.at[:, cols, :], out_hbm.at[:, cols, :], out_sem.at[slot_of(q, r, h)])

    bias_out = bo_v[...].astype(F32).reshape(1, LANES)

    def finish(update, q, r, h):
        cols = pl.ds(column_of(q, r, h), HALF)
        for g in range(8):
            for k in range(4):
                i = g * 4 + k
                part = update[g * HALF:(g + 1) * HALF, k * LANES:(k + 1) * LANES] + bias_out
                z_buf[i, cols, :] = (z_buf[i, cols, :].astype(F32) + part).astype(BF16)
        out_copy(q, r, h).start()

    def half_unit(q, r, h):
        slot = slot_of(q, r, h)
        for c in range(PIECES):
            outer_piece(slot, c)
        update = project_piece(0)
        for c in range(1, PIECES):
            update = update + project_piece(c)
        finish(update, q, r, h)

    z_copy.wait()
    for h in range(2):
        half_unit(0, 0, h)
    for h in range(2):
        for c in range(PIECES):
            arrived(slot_of(1, 0, h), c)
        half_unit(1, 0, h)
    for h in range(2):
        for c in range(PIECES):
            arrived(slot_of(0, 3, h), c)
            if h == 0:
                send(to_right(3, h, c))
            send(to_sib(3, h, c))
            arrived(slot_of(0, 1, h), c)
            if h == 1:
                send(to_left(1, h, c))
            send(to_sib(1, h, c))
        half_unit(0, 3, h)
        half_unit(0, 1, h)
        for r in (3, 1):
            for c in range(PIECES):
                arrived(slot_of(1, r, h), c)
            half_unit(1, r, h)
    for c in range(PIECES):
        for h in range(2):
            arrived(slot_of(0, 2, h), c)
            send(to_sib(2, h, c))
        for q in range(2):
            for h in range(2):
                slot = slot_of(q, 2, h)
                if q == 1:
                    arrived(slot, c)
                outer_piece(slot, c)
                part = project_piece(c)
                if c < PIECES - 1:
                    u_acc[q, h] = part if c == 0 else u_acc[q, h] + part
                else:
                    finish(u_acc[q, h] + part, q, 2, h)
    for copy in sent:
        copy.wait_send()
    for q in range(2):
        for r in range(4):
            for h in range(2):
                out_copy(q, r, h).wait()


def solution(mesh):
    row_spec = P(('batch', 'dap'))
    col_spec = P(None, ('batch', 'dap'))
    rep_spec = P()
    n_dev = mesh.shape['dap']

    def local_update(z_rows, msa, ln_scale, ln_offset, w_a, b_a, w_b, b_b, w_out, b_out):
        n_seq, n_loc, m_dim = msa.shape
        hid = w_a.shape[1]
        pair = z_rows.shape[2]
        x = jnp.transpose(msa, (1, 2, 0)).reshape(n_loc * m_dim, n_seq)
        rows_piece = HALF * hid // PIECES
        any_spec = pl.BlockSpec(memory_space=pl.ANY)
        vmem = pltpu.VMEM
        dma = pltpu.SemaphoreType.DMA
        return pl.pallas_call(
            functools.partial(kernel, n_dev),
            out_shape=jax.ShapeDtypeStruct(z_rows.shape, BF16),
            in_specs=[any_spec] * 10,
            out_specs=any_spec,
            scratch_shapes=[
                vmem(z_rows.shape, BF16), vmem(x.shape, BF16),
                vmem((m_dim,), BF16), vmem((m_dim,), BF16),
                vmem((hid, m_dim), BF16), vmem((hid,), BF16), vmem((hid, m_dim), BF16), vmem((hid,), BF16),
                vmem(w_out.shape, BF16), vmem((pair,), BF16),
                vmem((m_dim, LANES), F32), vmem((m_dim, LANES), F32),
                vmem((4 * hid, LANES), F32), vmem((HALF * hid, LANES), F32), vmem((hid, LANES), F32),
                vmem((4 * hid, 4 * m_dim), BF16), vmem((HALF * hid, HALF * m_dim), BF16),
                vmem((n_seq, n_loc * hid), BF16),
                vmem((16, PIECES, rows_piece, n_seq), BF16),
                vmem((PIECES, LANES, 8 * LANES), BF16),
                vmem(w_out.shape, F32), vmem((PIECES, 8 * LANES, 4 * pair), BF16),
                vmem((2, 2, LANES, 4 * pair), F32),
                dma((8,)), dma((n_loc // 4,)), dma, dma((16,)), dma((16, PIECES)),
                dma((3, PIECES)), dma((3, PIECES)), dma((8, PIECES)),
            ],
            compiler_params=pltpu.CompilerParams(collective_id=0, has_side_effects=True, vmem_limit_bytes=60 * 1024 * 1024),
            name='outer_mean_ring',
        )(z_rows, x, ln_scale, ln_offset, w_a.T, b_a, w_b.T, b_b, w_out, b_out)

    return jax.shard_map(local_update, mesh=mesh, in_specs=(row_spec, col_spec) + (rep_spec,) * 8, out_specs=row_spec, check_vma=False)
```

time: 98.5 us -> 50.1 us (0.51)
  waiting for transfers between devices: 49.1 us -> 0 us
  Pallas kernels: 0 us -> 46.8 us
  matrix products: 26.9 us -> 0 us
  between operations: 13.5 us -> 0.01 us
  other arithmetic: 7.44 us -> 0 us
  local copies, waits for them, and re-layouts: 1.34 us -> 3.14 us
    all_gather x1 -> x0, waiting for transfers between devices: 49 us -> none  [local_update(): full_b = lax.all_gather(proj_b, 'dap', axis=1, tiled=True)]
    pallas_call x0 -> x1, Pallas kernels: none -> 46.8 us  [local_update(): pl.pallas_call(functools.partial(kernel, n_dev), out_shape=jax.ShapeDtype...]
    dot_general x3 -> x0, matrix products: 26.9 us -> none  [the longest x1 23.4 us: tile_body(): jnp.einsum('icjd,cdz->ijz', outer_prod, w_cube, preferred_element_type=jn...]
    reduce_sum x2 -> x0, other arithmetic: 4.35 us -> none  [the longest x1 2.32 us: layer_norm(): var_val = jnp.mean(centred * centred, axis=-1, keepdims=True)]
    convert_element_type x6 -> x0, other arithmetic: 3.07 us -> none  [the longest x1 0.94 us: layer_norm(): (normed * ln_scale.astype(jnp.float32) + ln_offset.astype(jnp.float32)).a...]
    unnamed x14 -> x1, local copies, waits for them, and re-layouts: 1.34 us -> 3.14 us
  transfers between devices with their start and end apart: 1 -> 0, of which waited for: 1 -> 0; matrix products, arithmetic and copies ran while one was open for 2% -> 0% of each run, Pallas kernels for 0% -> 0%
where the time goes in v1:
time: 50.1 us; the launch traced here: 50 us
  Pallas kernels  46.8 us (93%)
  local copies, waits for them, and re-layouts  3.14 us (6%)
    pallas_call x1, Pallas kernels, local_update(): pl.pallas_call(functools.partial(kernel, n_dev), out_shape=jax.ShapeDtype...  46.8 us
    unnamed x1, local copies, waits for them, and re-layouts  3.14 us

profile of v1, /device:TPU:81, one launch (start us, length us, event | category | flops | bytes accessed | tf_op | source)
XLA Modules:
  0.0 50.0 jit_solution(13522291634264987028)
XLA Ops:
  0.0 46.8 %outer_mean_ring.1 = bf16[32,256,128]{2,1,0:T(8,128)(2,1)} custom-call(bf16[32,256,128]{2,1,0:T(8,128)(2,1)} %z_hbm.1, bf16[2048,512]{1,0:T(8,128)(2,1)} %bitcast.5, bf16[64]{0:T(256)(128)(2,1)} %ls_hbm.1, bf16[64]{0:T(256)(128)(2,1)} %lo_hbm.1, bf16[32,64]{1,0:T(8,128)(2,1)} %bitcast.6, bf16[32]{0:T(256)(128)(2,1)} %ba_hbm.1, bf16[32,64]{1,0:T(8,128)(2,1)} %bitcast.7, ...), custom_call_target="tpu_custom_call" | custom-call | tf_op jit(solution)/shard_map/outer_mean_ring/pallas_call | solution.py:280
  46.8 3.1 %copy.12 = bf16[32,256,128]{2,1,0:T(8,128)(2,1)} copy(bf16[32,256,128]{2,1,0:T(8,128)(2,1)} %outer_mean_ring.1) | data formatting | bytes 4194304

commit v2 on v1

--- a/solution.py
+++ b/solution.py
@@ -13,6 +13,10 @@
 LANES = 128
 HALF = 16
 PIECES = 4
+WHOLE = (0, 4)
+OWN = ((0, 2), (2, 4))
+FORWARD = ((0, 2), (2, 3), (3, 4))
+LAST = 12
 MESH = pl.DeviceIdType.MESH
 
 
@@ -26,10 +30,11 @@
     return jnp.broadcast_to(jnp.sum(picked, axis=1, keepdims=True), (count, LANES))
 
 
-def kernel(n_dev, z_hbm, x_hbm, ls_hbm, lo_hbm, wa_hbm, ba_hbm, wb_hbm, bb_hbm, wo_hbm, bo_hbm, out_hbm,
-           z_buf, x_buf, ls_v, lo_v, wa_v, ba_v, wb_v, bb_v, wo_v, bo_v,
-           scale_bc, offset_bc, bias_a, bias_b, row_bc, proj_a_w, proj_b_w, a_mat, bt, o_mat, w_f32, w_diag, u_acc,
-           small_sem, x_sem, z_sem, out_sem, recv_sem, right_sem, left_sem, sib_sem):
+def kernel(n_dev, z_hbm, x_hbm, ls_hbm, lo_hbm, wa_hbm, ba_hbm, wb_hbm, bb_hbm, wo_hbm, bo_hbm,
+           z_buf, a_mat, w_diag, u_last, bt_last,
+           x_buf, ls_v, lo_v, wa_v, ba_v, wb_v, bb_v, wo_v, bo_v,
+           scale_bc, offset_bc, bias_a, bias_b, row_bc, proj_a_w, proj_b_w, bt, o_mat, w_f32, u_acc,
+           small_sem, x_sem, z_sem, recv_sem, send_sem):
     n_seq = x_hbm.shape[1]
     n_loc = z_hbm.shape[0]
     m_dim = wa_hbm.shape[1]
@@ -94,39 +99,27 @@
 
     rows_piece = HALF * hid // PIECES
 
-    def remote(src, dst, send, recv, peer):
-        return pltpu.make_async_remote_copy(src_ref=src, dst_ref=dst, send_sem=send, recv_sem=recv,
-                                            device_id={'dap': peer}, device_id_type=MESH)
-
     def slot_of(q, r, h):
         return q * 8 + r * 2 + h
 
-    def to_right(r, h, c):
-        r_there = (r + 3) % 4
-        k = (0 if r == 0 else 2) + (h if r == 0 else 0)
-        return remote(bt.at[slot_of(0, r, h), c], bt.at[slot_of(0, r_there, h), c], right_sem.at[k, c],
-                      recv_sem.at[slot_of(0, r_there, h), c], right)
-
-    def to_left(r, h, c):
-        r_there = (r + 1) % 4
-        k = (0 if r == 0 else 2) + (h if r == 0 else 0)
-        return remote(bt.at[slot_of(0, r, h), c], bt.at[slot_of(0, r_there, h), c], left_sem.at[k, c],
-                      recv_sem.at[slot_of(0, r_there, h), c], left)
-
-    def to_sib(r, h, c):
-        return remote(bt.at[slot_of(0, r, h), c], bt.at[slot_of(1, r, h), c], sib_sem.at[r * 2 + h, c],
-                      recv_sem.at[slot_of(1, r, h), c], sib)
-
-    def arrived(slot, c):
-        remote(bt.at[slot, c], bt.at[slot, c], sib_sem.at[0, 0], recv_sem.at[slot, c], sib).wait_recv()
-
-    sent = []
-
-    def send(copy):
-        copy.start()
-        sent.append(copy)
-
-    bias_four = None
+    def view(slot, group):
+        if slot // 2 * 2 == LAST and group == FORWARD[-1]:
+            return bt_last.at[slot % 2]
+        return bt.at[slot, pl.ds(group[0], group[1] - group[0])]
+
+    arrivals = {}
+
+    def transfer(src, dst, group, peer):
+        sem = recv_sem.at[arrivals.setdefault((dst, group), len(arrivals))]
+        return pltpu.make_async_remote_copy(src_ref=view(src, group), dst_ref=view(dst, group), send_sem=send_sem,
+                                            recv_sem=sem, device_id={'dap': peer}, device_id_type=MESH)
+
+    def arrived(slot, group):
+        transfer(slot, slot, group, sib).wait_recv()
+
+    def send(src, dst, group, peer):
+        transfer(src, dst, group, peer).start()
+
     for h in range(2):
         for k in range(4):
             x_copies[h * 4 + k].wait()
@@ -144,10 +137,11 @@
             bt[slot_of(0, 0, h), c] = (res + bias).astype(BF16)
         if h == 0:
             pl.semaphore_wait(barrier, 3)
-        for c in range(PIECES):
-            send(to_right(0, h, c))
-            send(to_left(0, h, c))
-            send(to_sib(0, h, c))
+        own = slot_of(0, 0, h)
+        for group in OWN:
+            send(own, slot_of(0, 3, h), group, right)
+            send(own, slot_of(0, 1, h), group, left)
+        send(own, slot_of(1, 0, h), WHOLE, sib)
 
     for copy in small[4:]:
         copy.wait()
@@ -192,10 +186,6 @@
         src = lax.rem(chip + r, n_dev // 2) * 2 + (core if q == 0 else 1 - core)
         return pl.multiple_of(src * (2 * HALF) + h * HALF, HALF)
 
-    def out_copy(q, r, h):
-        cols = pl.ds(column_of(q, r, h), HALF)
-        return pltpu.make_async_copy(z_buf.at[:, cols, :], out_hbm.at[:, cols, :], out_sem.at[slot_of(q, r, h)])
-
     bias_out = bo_v[...].astype(F32).reshape(1, LANES)
 
     def finish(update, q, r, h):
@@ -205,7 +195,6 @@
                 i = g * 4 + k
                 part = update[g * HALF:(g + 1) * HALF, k * LANES:(k + 1) * LANES] + bias_out
                 z_buf[i, cols, :] = (z_buf[i, cols, :].astype(F32) + part).astype(BF16)
-        out_copy(q, r, h).start()
 
     def half_unit(q, r, h):
         slot = slot_of(q, r, h)
@@ -220,46 +209,88 @@
     for h in range(2):
         half_unit(0, 0, h)
     for h in range(2):
-        for c in range(PIECES):
-            arrived(slot_of(1, 0, h), c)
+        arrived(slot_of(1, 0, h), WHOLE)
         half_unit(1, 0, h)
     for h in range(2):
-        for c in range(PIECES):
-            arrived(slot_of(0, 3, h), c)
-            if h == 0:
-                send(to_right(3, h, c))
-            send(to_sib(3, h, c))
-            arrived(slot_of(0, 1, h), c)
-            if h == 1:
-                send(to_left(1, h, c))
-            send(to_sib(1, h, c))
-        half_unit(0, 3, h)
-        half_unit(0, 1, h)
+        for group in OWN:
+            arrived(slot_of(0, 3, h), group)
+            arrived(slot_of(0, 1, h), group)
+            for piece in FORWARD:
+                if group[0] <= piece[0] < group[1]:
+                    if h == 0:
+                        send(slot_of(0, 3, 0), slot_of(0, 2, 0), piece, right)
+                    else:
+                        send(slot_of(0, 1, 1), slot_of(0, 2, 1), piece, left)
         for r in (3, 1):
-            for c in range(PIECES):
-                arrived(slot_of(1, r, h), c)
+            send(slot_of(0, r, h), slot_of(1, r, h), WHOLE, sib)
+        for r in (3, 1):
+            half_unit(0, r, h)
+        for r in (3, 1):
+            arrived(slot_of(1, r, h), WHOLE)
             half_unit(1, r, h)
-    for c in range(PIECES):
+
+    def part_unit(q, h, group):
+        for c in range(*group):
+            outer_piece(slot_of(q, 2, h), c)
+        update = project_piece(group[0])
+        for c in range(group[0] + 1, group[1]):
+            update = update + project_piece(c)
+        return update
+
+    for group in FORWARD:
+        first, last = group == FORWARD[0], group == FORWARD[-1]
         for h in range(2):
-            arrived(slot_of(0, 2, h), c)
-            send(to_sib(2, h, c))
-        for q in range(2):
-            for h in range(2):
-                slot = slot_of(q, 2, h)
-                if q == 1:
-                    arrived(slot, c)
-                outer_piece(slot, c)
-                part = project_piece(c)
-                if c < PIECES - 1:
-                    u_acc[q, h] = part if c == 0 else u_acc[q, h] + part
-                else:
-                    finish(u_acc[q, h] + part, q, 2, h)
-    for copy in sent:
-        copy.wait_send()
-    for q in range(2):
-        for r in range(4):
-            for h in range(2):
-                out_copy(q, r, h).wait()
+            arrived(slot_of(0, 2, h), group)
+            send(slot_of(0, 2, h), slot_of(1, 2, h), group, sib)
+        for h in range(2):
+            update = part_unit(0, h, group)
+            if last:
+                finish(u_acc[h] + update, 0, 2, h)
+            else:
+                u_acc[h] = update if first else u_acc[h] + update
+        for h in range(2):
+            arrived(slot_of(1, 2, h), group)
+            if not last:
+                update = part_unit(1, h, group)
+                if first:
+                    update = update + jnp.concatenate([bias_out] * 4, axis=1)
+                u_last[h] = update if first else u_last[h] + update
+    pltpu.make_async_remote_copy(src_ref=bt.at[pl.ds(0, 14)], dst_ref=bt.at[pl.ds(0, 14)], send_sem=send_sem,
+                                 recv_sem=recv_sem.at[0], device_id={'dap': sib}, device_id_type=MESH).wait_send()
+
+
+def last_kernel(n_dev, z_buf, a_mat, w_diag, u_last, bt_last, out_hbm, cols_buf, sem):
+    width = 2 * HALF
+    inv_seq = 1.0 / a_mat.shape[0]
+    me = lax.axis_index('dap')
+    chips = n_dev // 2
+    mine = lax.rem(me // 2 + 2, chips) * 2 + 1 - lax.rem(me, 2)
+
+    def block(k):
+        return pl.ds(pl.multiple_of(lax.rem(mine + k, n_dev) * width, width), width)
+
+    copies = [pltpu.make_async_copy(z_buf.at[:, block(k), :], out_hbm.at[:, block(k), :], sem.at[k]) for k in range(1, n_dev)]
+    for copy in copies:
+        copy.start()
+    c = PIECES - 1
+    for h in range(2):
+        res = jnp.dot(bt_last[h, 0], a_mat[...], preferred_element_type=F32)
+        res = (res * inv_seq).astype(BF16)
+        wide = jnp.concatenate(
+            [jnp.concatenate([res[d * HALF:(d + 1) * HALF, g * LANES:(g + 1) * LANES] for d in range(8)], axis=1)
+             for g in range(8)], axis=0)
+        update = u_last[h] + jnp.dot(wide, w_diag[c], preferred_element_type=F32)
+        cols = pl.ds(pl.multiple_of(mine * width + h * HALF, HALF), HALF)
+        for g in range(8):
+            for k in range(4):
+                i = g * 4 + k
+                part = update[g * HALF:(g + 1) * HALF, k * LANES:(k + 1) * LANES]
+                cols_buf[i, h * HALF:(h + 1) * HALF, :] = (z_buf[i, cols, :].astype(F32) + part).astype(BF16)
+    copy = pltpu.make_async_copy(cols_buf, out_hbm.at[:, block(0), :], sem.at[0])
+    copy.start()
+    copies.append(copy)
+    for copy in copies:
+        copy.wait()
 
 
 def solution(mesh):
@@ -277,29 +308,42 @@
         any_spec = pl.BlockSpec(memory_space=pl.ANY)
         vmem = pltpu.VMEM
         dma = pltpu.SemaphoreType.DMA
-        return pl.pallas_call(
+        outs = [
+            vmem(z_rows.shape, BF16), vmem((n_seq, n_loc * hid), BF16), vmem((PIECES, 8 * LANES, 4 * pair), BF16),
+            vmem((2, LANES, 4 * pair), F32), vmem((2, 1, rows_piece, n_seq), BF16),
+        ]
+        vmem_spec = pl.BlockSpec(memory_space=pltpu.VMEM)
+        made = pl.pallas_call(
             functools.partial(kernel, n_dev),
-            out_shape=jax.ShapeDtypeStruct(z_rows.shape, BF16),
+            out_shape=outs,
             in_specs=[any_spec] * 10,
-            out_specs=any_spec,
+            out_specs=[vmem_spec] * len(outs),
             scratch_shapes=[
-                vmem(z_rows.shape, BF16), vmem(x.shape, BF16),
+                vmem(x.shape, BF16),
                 vmem((m_dim,), BF16), vmem((m_dim,), BF16),
                 vmem((hid, m_dim), BF16), vmem((hid,), BF16), vmem((hid, m_dim), BF16), vmem((hid,), BF16),
                 vmem(w_out.shape, BF16), vmem((pair,), BF16),
                 vmem((m_dim, LANES), F32), vmem((m_dim, LANES), F32),
                 vmem((4 * hid, LANES), F32), vmem((HALF * hid, LANES), F32), vmem((hid, LANES), F32),
                 vmem((4 * hid, 4 * m_dim), BF16), vmem((HALF * hid, HALF * m_dim), BF16),
-                vmem((n_seq, n_loc * hid), BF16),
                 vmem((16, PIECES, rows_piece, n_seq), BF16),
                 vmem((PIECES, LANES, 8 * LANES), BF16),
-                vmem(w_out.shape, F32), vmem((PIECES, 8 * LANES, 4 * pair), BF16),
-                vmem((2, 2, LANES, 4 * pair), F32),
-                dma((8,)), dma((n_loc // 4,)), dma, dma((16,)), dma((16, PIECES)),
-                dma((3, PIECES)), dma((3, PIECES)), dma((8, PIECES)),
+                vmem(w_out.shape, F32),
+                vmem((2, LANES, 4 * pair), F32),
+                dma((8,)), dma((n_loc // 4,)), dma, dma((26,)), dma,
             ],
-            compiler_params=pltpu.CompilerParams(collective_id=0, has_side_effects=True, vmem_limit_bytes=60 * 1024 * 1024),
+            compiler_params=pltpu.CompilerParams(collective_id=0, has_side_effects=True, vmem_limit_bytes=44 * 1024 * 1024),
             name='outer_mean_ring',
         )(z_rows, x, ln_scale, ln_offset, w_a.T, b_a, w_b.T, b_b, w_out, b_out)
+        made = [pltpu.with_memory_space_constraint(part, pltpu.VMEM) for part in made]
+        return pl.pallas_call(
+            functools.partial(last_kernel, n_dev),
+            out_shape=jax.ShapeDtypeStruct(z_rows.shape, BF16),
+            in_specs=[vmem_spec] * len(outs),
+            out_specs=any_spec,
+            scratch_shapes=[vmem((n_loc, 2 * HALF, pair), BF16), dma((n_dev,))],
+            compiler_params=pltpu.CompilerParams(vmem_limit_bytes=8 * 1024 * 1024),
+            name='outer_mean_last',
+        )(*made)
 
     return jax.shard_map(local_update, mesh=mesh, in_specs=(row_spec, col_spec) + (rep_spec,) * 8, out_specs=row_spec, check_vma=False)

time: 50.1 us -> 51.7 us (1.032)
  local copies, waits for them, and re-layouts: 3.14 us -> 5.62 us
  Pallas kernels: 46.8 us -> 45.7 us
    unnamed x1 -> x16, local copies, waits for them, and re-layouts: 3.14 us -> 5.62 us
    pallas_call x1 -> x2, Pallas kernels: 46.8 us -> 45.7 us  [the longest x1 43.5 us: local_update(): pl.pallas_call(functools.partial(kernel, n_dev), out_shape=outs, in_specs...]
where the time goes in v2:
time: 51.7 us; the launch traced here: 51.5 us
  Pallas kernels  45.7 us (88%)
  local copies, waits for them, and re-layouts  5.62 us (11%)
    pallas_call x1, Pallas kernels, local_update(): pl.pallas_call(functools.partial(kernel, n_dev), out_shape=outs, in_specs...  43.5 us
    unnamed x16, local copies, waits for them, and re-layouts  5.62 us
    pallas_call x1, Pallas kernels, local_update(): pl.pallas_call(functools.partial(last_kernel, n_dev), out_shape=jax.Shape...  2.16 us

profile of v2, /device:TPU:81, one launch (start us, length us, event | category | flops | bytes accessed | tf_op | source)
XLA Modules:
  0.0 51.5 jit_solution(16886119227279806083)
XLA Ops:
  0.0 0.0 copy-start
  0.0 0.9 %copy-done = bf16[1024,128]{1,0:T(8,128)(2,1)S(1)} copy-done((bf16[1024,128]{1,0:T(8,128)(2,1)S(1)}, bf16[1024,128]{1,0:T(8,128)(2,1)}, u32[]{:S(2)}) %copy-start) | copy-done | bytes 262168
  1.0 0.0 copy-start.1
  1.0 0.7 %copy-done.1 = bf16[64,32]{0,1:T(8,128)(2,1)S(1)} copy-done((bf16[64,32]{0,1:T(8,128)(2,1)S(1)}, bf16[64,32]{0,1:T(8,128)(2,1)}, u32[]{:S(2)}) %copy-start.1) | copy-done | bytes 4120
  1.6 0.0 copy-start.2
  1.7 0.7 %copy-done.2 = bf16[64,32]{0,1:T(8,128)(2,1)S(1)} copy-done((bf16[64,32]{0,1:T(8,128)(2,1)S(1)}, bf16[64,32]{0,1:T(8,128)(2,1)}, u32[]{:S(2)}) %copy-start.2) | copy-done | bytes 4120
  2.3 0.0 copy-start.3
  2.3 0.7 %copy-done.3 = bf16[64]{0:T(256)(128)(2,1)S(1)} copy-done((bf16[64]{0:T(256)(128)(2,1)S(1)}, bf16[64]{0:T(256)(128)(2,1)}, u32[]{:S(2)}) %copy-start.3) | copy-done | bytes 152
  3.0 0.0 copy-start.4
  3.0 0.7 %copy-done.4 = bf16[64]{0:T(256)(128)(2,1)S(1)} copy-done((bf16[64]{0:T(256)(128)(2,1)S(1)}, bf16[64]{0:T(256)(128)(2,1)}, u32[]{:S(2)}) %copy-start.4) | copy-done | bytes 152
  3.7 0.0 copy-start.5
  3.7 0.7 %copy-done.5 = bf16[32]{0:T(256)(128)(2,1)S(1)} copy-done((bf16[32]{0:T(256)(128)(2,1)S(1)}, bf16[32]{0:T(256)(128)(2,1)}, u32[]{:S(2)}) %copy-start.5) | copy-done | bytes 88
  4.3 0.0 copy-start.6
  4.3 0.7 %copy-done.6 = bf16[32]{0:T(256)(128)(2,1)S(1)} copy-done((bf16[32]{0:T(256)(128)(2,1)S(1)}, bf16[32]{0:T(256)(128)(2,1)}, u32[]{:S(2)}) %copy-start.6) | copy-done | bytes 88
  5.0 0.0 copy-start.7
  5.0 0.7 %copy-done.7 = bf16[128]{0:T(256)(128)(2,1)S(1)} copy-done((bf16[128]{0:T(256)(128)(2,1)S(1)}, bf16[128]{0:T(256)(128)(2,1)}, u32[]{:S(2)}) %copy-start.7) | copy-done | bytes 280
  5.6 43.5 %outer_mean_ring.1 = (bf16[32,256,128]{2,1,0:T(8,128)(2,1)S(1)}, bf16[512,1024]{1,0:T(8,128)(2,1)S(1)}, bf16[4,1024,512]{2,1,0:T(8,128)(2,1)S(1)}, f32[2,128,512...) custom-call(bf16[32,256,128]{2,1,0:T(8,128)(2,1)} %z_hbm.1, bf16[2048,512]{1,0:T(8,128)(2,1)} %bitcast.7, ...), custom_call_target="tpu_custom_call" | custom-call | tf_op jit(solution)/shard_map/outer_mean_ring/pallas_call | solution.py:316
  49.1 2.2 %outer_mean_last.1 = bf16[32,256,128]{2,1,0:T(8,128)(2,1)} custom-call(bf16[32,256,128]{2,1,0:T(8,128)(2,1)S(1)} %get-tuple-element.10.z_buf, bf16[512,1024]{1,0:T(8,128)(2,1)S(1)} %get-tuple-element.11.a_mat, bf16[4,1024,512]{2,1,0:T(8,128)(2,1)S(1)} %get-tuple-element.12.w_diag, f32[2,128,512]{2,1,0:T(8,128)S(1)} %get-tuple-element.13.u_last, ...), custom_call_target="tpu_custom_call" | custom-call | tf_op jit(solution)/shard_map/outer_mean_last/pallas_call | solution.py:339
Async XLA Ops:
  0.0 0.9 %copy-start = (bf16[1024,128]{1,0:T(8,128)(2,1)S(1)}, bf16[1024,128]{1,0:T(8,128)(2,1)}, u32[]{:S(2)}) copy-start(bf16[1024,128]{1,0:T(8,128)(2,1)} %wo_hbm.1) | copy-start | bytes 786436
  1.0 0.7 %copy-start.1 = (bf16[64,32]{0,1:T(8,128)(2,1)S(1)}, bf16[64,32]{0,1:T(8,128)(2,1)}, u32[]{:S(2)}) copy-start(bf16[64,32]{0,1:T(8,128)(2,1)} %param.14) | copy-start | bytes 12292
  1.6 0.7 %copy-start.2 = (bf16[64,32]{0,1:T(8,128)(2,1)S(1)}, bf16[64,32]{0,1:T(8,128)(2,1)}, u32[]{:S(2)}) copy-start(bf16[64,32]{0,1:T(8,128)(2,1)} %param.16) | copy-start | bytes 12292
  2.3 0.7 %copy-start.3 = (bf16[64]{0:T(256)(128)(2,1)S(1)}, bf16[64]{0:T(256)(128)(2,1)}, u32[]{:S(2)}) copy-start(bf16[64]{0:T(256)(128)(2,1)} %ls_hbm.1) | copy-start | bytes 388
  3.0 0.7 %copy-start.4 = (bf16[64]{0:T(256)(128)(2,1)S(1)}, bf16[64]{0:T(256)(128)(2,1)}, u32[]{:S(2)}) copy-start(bf16[64]{0:T(256)(128)(2,1)} %lo_hbm.1) | copy-start | bytes 388
  3.7 0.7 %copy-start.5 = (bf16[32]{0:T(256)(128)(2,1)S(1)}, bf16[32]{0:T(256)(128)(2,1)}, u32[]{:S(2)}) copy-start(bf16[32]{0:T(256)(128)(2,1)} %ba_hbm.1) | copy-start | bytes 196
  4.3 0.7 %copy-start.6 = (bf16[32]{0:T(256)(128)(2,1)S(1)}, bf16[32]{0:T(256)(128)(2,1)}, u32[]{:S(2)}) copy-start(bf16[32]{0:T(256)(128)(2,1)} %bb_hbm.1) | copy-start | bytes 196
  5.0 0.7 %copy-start.7 = (bf16[128]{0:T(256)(128)(2,1)S(1)}, bf16[128]{0:T(256)(128)(2,1)}, u32[]{:S(2)}) copy-start(bf16[128]{0:T(256)(128)(2,1)} %bo_hbm.1) | copy-start | bytes 772

commit v3 on v2

v3 whole, which is shorter than its diff:
```python
import functools

import jax
import jax.numpy as jnp
from jax import lax
from jax.experimental import pallas as pl
from jax.experimental.pallas import tpu as pltpu
from jax.sharding import PartitionSpec as P

LN_EPS = 1e-5
F32 = jnp.float32
BF16 = jnp.bfloat16
LANES = 128
HALF = 16
PIECES = 4
BLOCK = 128
ALL = ('rows', 0, 4)
FIRST_OWN = (('lanes', 0), ('lanes', 1))
SECOND_OWN = (('rows', 0, 2), ('rows', 2, 4))
SHARED = (('rows', 0, 2), ('rows', 2, 3))
FINAL = ('rows', 3, 4)
MESH = pl.DeviceIdType.MESH


def iota(shape, dim):
    return lax.broadcasted_iota(jnp.int32, shape, dim)


def column_lanes(row, count):
    spread = jnp.broadcast_to(row, (count, count))
    picked = jnp.where(iota((count, count), 0) == iota((count, count), 1), spread, 0.0)
    return jnp.broadcast_to(jnp.sum(picked, axis=1, keepdims=True), (count, LANES))


def kernel(n_dev, z_hbm, x_hbm, ls_hbm, lo_hbm, wa_hbm, ba_hbm, wb_hbm, bb_hbm, wo_hbm, bo_hbm,
           z_buf, a_mat, w_last, u_last, bt_last,
           x_buf, ls_v, lo_v, wa_v, ba_v, wb_v, bb_v, wo_v, bo_v,
           scale_bc, offset_bc, bias_a, bias_b, row_bc, proj_a_w, proj_b_w, bt, o_mat, w_f32, w_diag,
           small_sem, x_sem, z_sem, recv_sem, send_sem):
    n_seq = x_hbm.shape[1]
    n_loc = z_hbm.shape[0]
    m_dim = wa_hbm.shape[1]
    hid = wa_hbm.shape[0]
    inv_seq = 1.0 / n_seq
    me = lax.axis_index('dap')
    core = lax.rem(me, 2)
    sib = me + 1 - 2 * core
    right = lax.rem(me + 2, n_dev)
    left = lax.rem(me + n_dev - 2, n_dev)

    barrier = pltpu.get_barrier_semaphore()
    for peer in (sib, right, left):
        pl.semaphore_signal(barrier, inc=1, device_id={'dap': peer}, device_id_type=MESH)

    small = [pltpu.make_async_copy(src, dst, small_sem.at[k]) for k, (src, dst) in enumerate((
        (wb_hbm, wb_v), (bb_hbm, bb_v), (ls_hbm, ls_v), (lo_hbm, lo_v), (wa_hbm, wa_v), (ba_hbm, ba_v),
        (wo_hbm, wo_v), (bo_hbm, bo_v)))]
    half_rows = HALF * m_dim
    half_seq = n_seq // 2
    parts = [(slice(k * half_rows // 2, (k + 1) * half_rows // 2), slice(p * half_seq, (p + 1) * half_seq))
             for p in range(2) for k in range(2)]
    parts += [(slice(half_rows + k * half_rows // 2, half_rows + (k + 1) * half_rows // 2), slice(0, n_seq)) for k in range(2)]
    x_copies = [pltpu.make_async_copy(x_hbm.at[part], x_buf.at[part], x_sem.at[k]) for k, part in enumerate(parts)]
    for copy in x_copies[:2] + small[:4] + x_copies[2:4]:
        copy.start()
    z_copy = pltpu.make_async_copy(z_hbm, z_buf, z_sem)

    for copy in small[:4]:
        copy.wait()
    row_bc[...] = column_lanes(bb_v[...].astype(F32).reshape(1, hid), hid)
    wb_rows = wb_v[...].astype(F32)
    wb_two = jnp.concatenate([wb_rows, wb_rows], axis=1)
    scale_bc[...] = column_lanes(ls_v[...].astype(F32).reshape(1, m_dim), m_dim)
    offset_bc[...] = column_lanes(lo_v[...].astype(F32).reshape(1, m_dim), m_dim)
    in_half = iota((HALF, LANES), 0)
    in_pair = iota((HALF, LANES), 1) // m_dim
    for d in range(hid):
        spread = jnp.broadcast_to(wb_two[d:d + 1, :], (HALF, LANES))
        for t in range(HALF * m_dim // LANES):
            part = jnp.where(in_half == in_pair + 2 * t, spread, 0.0)
            proj_b_w[d * HALF:(d + 1) * HALF, t * LANES:(t + 1) * LANES] = part.astype(BF16)
        bias_b[d * HALF:(d + 1) * HALF, :] = jnp.broadcast_to(row_bc[d:d + 1, :], (HALF, LANES))

    def norm_part(rows, lanes):
        width = lanes.stop - lanes.start
        scale = jnp.concatenate([scale_bc[...]] * (width // LANES), axis=1)
        offset = jnp.concatenate([offset_bc[...]] * (width // LANES), axis=1)

        def body(n, carry):
            at = (pl.ds(pl.multiple_of(rows.start + n * m_dim, m_dim), m_dim), lanes)
            value = x_buf[at].astype(F32)
            mean = jnp.sum(value, axis=0, keepdims=True) * (1.0 / m_dim)
            centred = value - mean
            var = jnp.sum(centred * centred, axis=0, keepdims=True) * (1.0 / m_dim)
            normed = centred * lax.rsqrt(var + LN_EPS)
            x_buf[at] = (normed * scale + offset).astype(BF16)
            return carry

        lax.fori_loop(0, (rows.stop - rows.start) // m_dim, body, 0, unroll=4)

    def slot_of(q, r, h):
        return q * 8 + r * 2 + h

    def view(q, r, h, group):
        slot = slot_of(q, r, h)
        if group[0] == 'lanes':
            return bt.at[slot, group[1]]
        if r == 2 and group == FINAL and q == 1:
            return bt_last.at[h]
        if group == ALL:
            return bt.at[slot]
        return bt.at[slot, :, pl.ds(group[1] * BLOCK, (group[2] - group[1]) * BLOCK), :]

    sems = {}

    def transfer(q, r, h, group, peer, r_there):
        if r_there == 2:
            k = SHARED.index(group) if group != FINAL else 2
        else:
            k = 0 if group in (ALL, FIRST_OWN[0], SECOND_OWN[0]) else 1
        k = sems.setdefault((r_there, h, k), len(sems))
        return pltpu.make_async_remote_copy(
            src_ref=view(q, r, h, group), dst_ref=view(q, r_there, h, group), send_sem=send_sem,
            recv_sem=recv_sem.at[q * 16 + k], device_id={'dap': peer}, device_id_type=MESH)

    def arrived(q, r, h, group):
        transfer(q, r, h, group, sib, r).wait_recv()

    def to_right(q, r, h, group):
        transfer(q, r, h, group, right, (r + 3) % 4).start()

    def to_left(q, r, h, group):
        transfer(q, r, h, group, left, (r + 1) % 4).start()

    def to_sib(q, r, h, group):
        transfer(q, r, h, group, sib, r).start()

    own, other = core, 1 - core

    def project_b(h, c, lanes):
        rows = slice(c * BLOCK, (c + 1) * BLOCK)
        width = lanes.stop - lanes.start
        res = jnp.dot(proj_b_w[rows, :], x_buf[h * half_rows:(h + 1) * half_rows, lanes], preferred_element_type=F32)
        res = (res + jnp.concatenate([bias_b[rows, :]] * (width // LANES), axis=1)).astype(BF16)
        for k in range(width // half_seq):
            bt[slot_of(own, 0, h), lanes.start // half_seq + k, rows, :] = res[:, k * half_seq:(k + 1) * half_seq]

    for p in range(2):
        for k in range(2):
            x_copies[2 * p + k].wait()
            norm_part(*parts[2 * p + k])
        if p == 0:
            for copy in x_copies[4:] + small[4:] + [z_copy]:
                copy.start()
        for c in range(PIECES):
            project_b(0, c, parts[2 * p][1])
        if p == 0:
            pl.semaphore_wait(barrier, 3)
        to_right(own, 0, 0, FIRST_OWN[p])
        to_left(own, 0, 0, FIRST_OWN[p])
    to_sib(own, 0, 0, ALL)
    for k in range(2):
        x_copies[4 + k].wait()
        norm_part(*parts[4 + k])
    for group in SECOND_OWN:
        for c in range(*group[1:]):
            project_b(1, c, parts[4][1])
        to_right(own, 0, 1, group)
        to_left(own, 0, 1, group)
    to_sib(own, 0, 1, ALL)

    for copy in small[4:]:
        copy.wait()
    row_bc[...] = column_lanes(ba_v[...].astype(F32).reshape(1, hid), hid)
    bias_a[...] = jnp.concatenate([row_bc[...]] * 4, axis=0)
    wa_rows = wa_v[...].astype(F32)
    wa_wide = jnp.concatenate([jnp.concatenate([wa_rows] * 4, axis=1)] * 4, axis=0)
    same = (iota(wa_wide.shape, 0) // hid) == (iota(wa_wide.shape, 1) // m_dim)
    proj_a_w[...] = jnp.where(same, wa_wide, 0.0).astype(BF16)
    for g in range(n_loc // 4):
        res = jnp.dot(proj_a_w[...], x_buf[g * 4 * m_dim:(g + 1) * 4 * m_dim, :], preferred_element_type=F32)
        res = res + jnp.concatenate([bias_a[...]] * (n_seq // LANES), axis=1)
        a_mat[:, g * LANES:(g + 1) * LANES] = res.T.astype(BF16)

    w_f32[...] = wo_v[...].astype(F32)
    w_diag[...] = jnp.zeros_like(w_diag)
    w_last[...] = jnp.zeros_like(w_last)

    def spread_w(d, at):
        block = w_f32[pl.ds(d, hid, stride=hid), :].astype(BF16)
        for k in range(4):
            row = pl.multiple_of(lax.rem(d, 8) * LANES + k * hid, hid)
            at[pl.ds(row, hid), k * LANES:(k + 1) * LANES] = block

    for c in range(PIECES):
        at = w_diag.at[c] if c < PIECES - 1 else w_last

        def body(d, carry):
            spread_w(d, at)
            return carry

        lax.fori_loop(c * 8, (c + 1) * 8, body, 0)

    def outer_piece(slot, c):
        rows = slice(c * BLOCK, (c + 1) * BLOCK)
        lhs = jnp.concatenate([bt[slot, 0, rows, :], bt[slot, 1, rows, :]], axis=1)
        res = jnp.dot(lhs, a_mat[...], preferred_element_type=F32)
        res = (res * inv_seq).astype(BF16)
        for d in range(8):
            for g in range(8):
                o_mat[c, g * HALF:(g + 1) * HALF, d * LANES:(d + 1) * LANES] = (
                    res[d * HALF:(d + 1) * HALF, g * LANES:(g + 1) * LANES])

    def project_piece(c):
        return jnp.dot(o_mat[c], w_diag[c] if c < PIECES - 1 else w_last[...], preferred_element_type=F32)

    chip = me // 2

    def column_of(q, r, h):
        src = lax.rem(chip + r, n_dev // 2) * 2 + q
        return pl.multiple_of(src * (2 * HALF) + h * HALF, HALF)

    bias_out = bo_v[...].astype(F32).reshape(1, LANES)

    def finish(update, bias, q, r, h):
        cols = pl.ds(column_of(q, r, h), HALF)
        for g in range(8):
            for k in range(4):
                i = g * 4 + k
                part = update[g * HALF:(g + 1) * HALF, k * LANES:(k + 1) * LANES]
                if bias is not None:
                    part = part + bias
                z_buf[i, cols, :] = (z_buf[i, cols, :].astype(F32) + part).astype(BF16)

    def half_unit(q, r, h):
        slot = slot_of(q, r, h)
        for c in range(PIECES):
            outer_piece(slot, c)
        update = project_piece(0)
        for c in range(1, PIECES):
            update = update + project_piece(c)
        finish(update, bias_out, q, r, h)

    z_copy.wait()
    for h in range(2):
        half_unit(own, 0, h)
    for h in range(2):
        arrived(other, 0, h, ALL)
        half_unit(other, 0, h)
    for h in range(2):
        for k, group in enumerate(FIRST_OWN if h == 0 else SECOND_OWN):
            arrived(own, 3, h, group)
            arrived(own, 1, h, group)
            if h == 1:
                to_left(own, 1, 1, SHARED[k])
        if h == 0:
            for group in SHARED:
                to_right(own, 3, 0, group)
        for r in (3, 1):
            to_sib(own, r, h, ALL)
        for r in (3, 1):
            half_unit(own, r, h)
        for r in (3, 1):
            arrived(other, r, h, ALL)

        @pl.when(core == 1)
        def _():
            for q in range(2):
                if h == 0:
                    to_right(q, 3, 0, FINAL)
                else:
                    to_left(q, 1, 1, FINAL)

        for r in (3, 1):
            half_unit(other, r, h)

    def part_unit(q, h, group):
        slot = slot_of(q, 2, h)
        for c in range(*group[1:]):
            outer_piece(slot, c)
        update = project_piece(group[1])
        for c in range(group[1] + 1, group[2]):
            update = update + project_piece(c)
        return update

    wide_bias = jnp.concatenate([bias_out] * 4, axis=1)
    for group in SHARED:
        for h in range(2):
            arrived(own, 2, h, group)
            to_sib(own, 2, h, group)
        for q in (own, other):
            for h in range(2):
                if q is other:
                    arrived(other, 2, h, group)
                update = part_unit(q, h, group)
                u_last[q, h] = update + wide_bias if group is SHARED[0] else u_last[q, h] + update
    for h in range(2):
        arrived(0, 2, h, FINAL)

        @pl.when(core == 1)
        def _():
            to_sib(0, 2, h, FINAL)

    for h in range(2):
        finish(u_last[0, h] + part_unit(0, h, FINAL), None, 0, 2, h)
    for h in range(2):
        arrived(1, 2, h, FINAL)

        @pl.when(core == 1)
        def _():
            to_sib(1, 2, h, FINAL)

    for q, slots in enumerate((13, 15)):
        @pl.when(core == q)
        def _():
            everything = bt.at[pl.ds(0, slots)]
            pltpu.make_async_remote_copy(src_ref=everything, dst_ref=everything, send_sem=send_sem, recv_sem=recv_sem.at[0],
                                         device_id={'dap': sib}, device_id_type=MESH).wait_send()


def last_kernel(n_dev, z_buf, a_mat, w_last, u_last, bt_last, out_hbm, cols_buf, sem):
    width = 2 * HALF
    inv_seq = 1.0 / a_mat.shape[0]
    me = lax.axis_index('dap')
    chips = n_dev // 2
    mine = lax.rem(me // 2 + 2, chips) * 2 + 1

    def block(k):
        return pl.ds(pl.multiple_of(lax.rem(mine + k, n_dev) * width, width), width)

    copies = [pltpu.make_async_copy(z_buf.at[:, block(k), :], out_hbm.at[:, block(k), :], sem.at[k]) for k in range(1, n_dev)]
    for copy in copies:
        copy.start()
    lhs = jnp.concatenate([jnp.concatenate([bt_last[h, 0], bt_last[h, 1]], axis=1) for h in range(2)], axis=0)
    res = jnp.dot(lhs, a_mat[...], preferred_element_type=F32)
    res = (res * inv_seq).astype(BF16)
    wide = jnp.concatenate(
        [jnp.concatenate([res[h * BLOCK + d * HALF:h * BLOCK + (d + 1) * HALF, g * LANES:(g + 1) * LANES] for d in range(8)], axis=1)
         for h in range(2) for g in range(8)], axis=0)
    update = jnp.dot(wide, w_last[...], preferred_element_type=F32)
    for h in range(2):
        cols = pl.ds(pl.multiple_of(mine * width + h * HALF, HALF), HALF)
        for g in range(8):
            for k in range(4):
                i = g * 4 + k
                rows, lanes = slice(g * HALF, (g + 1) * HALF), slice(k * LANES, (k + 1) * LANES)
                part = u_last[1, h, rows, lanes] + update[h * BLOCK + g * HALF:h * BLOCK + (g + 1) * HALF, lanes]
                cols_buf[i, h * HALF:(h + 1) * HALF, :] = (z_buf[i, cols, :].astype(F32) + part).astype(BF16)
    copy = pltpu.make_async_copy(cols_buf, out_hbm.at[:, block(0), :], sem.at[0])
    copy.start()
    copies.append(copy)
    for copy in copies:
        copy.wait()


def solution(mesh):
    row_spec = P(('batch', 'dap'))
    col_spec = P(None, ('batch', 'dap'))
    rep_spec = P()
    n_dev = mesh.shape['dap']

    def local_update(z_rows, msa, ln_scale, ln_offset, w_a, b_a, w_b, b_b, w_out, b_out):
        n_seq, n_loc, m_dim = msa.shape
        hid = w_a.shape[1]
        pair = z_rows.shape[2]
        x = jnp.transpose(msa, (1, 2, 0)).reshape(n_loc * m_dim, n_seq)
        any_spec = pl.BlockSpec(memory_space=pltpu.HBM)
        vmem = pltpu.VMEM
        dma = pltpu.SemaphoreType.DMA
        outs = [
            vmem(z_rows.shape, BF16), vmem((n_seq, n_loc * hid), BF16), vmem((8 * LANES, 4 * pair), BF16),
            vmem((2, 2, LANES, 4 * pair), F32), vmem((2, 2, BLOCK, n_seq // 2), BF16),
        ]
        vmem_spec = pl.BlockSpec(memory_space=pltpu.VMEM)
        made = pl.pallas_call(
            functools.partial(kernel, n_dev),
            out_shape=outs,
            in_specs=[any_spec] * 10,
            out_specs=[vmem_spec] * len(outs),
            scratch_shapes=[
                vmem(x.shape, BF16),
                vmem((m_dim,), BF16), vmem((m_dim,), BF16),
                vmem((hid, m_dim), BF16), vmem((hid,), BF16), vmem((hid, m_dim), BF16), vmem((hid,), BF16),
                vmem(w_out.shape, BF16), vmem((pair,), BF16),
                vmem((m_dim, LANES), F32), vmem((m_dim, LANES), F32),
                vmem((4 * hid, LANES), F32), vmem((HALF * hid, LANES), F32), vmem((hid, LANES), F32),
                vmem((4 * hid, 4 * m_dim), BF16), vmem((HALF * hid, HALF * m_dim), BF16),
                vmem((16, 2, PIECES * BLOCK, n_seq // 2), BF16),
                vmem((PIECES, LANES, 8 * LANES), BF16),
                vmem(w_out.shape, F32), vmem((PIECES - 1, 8 * LANES, 4 * pair), BF16),
                dma((8,)), dma((6,)), dma, dma((32,)), dma,
            ],
            compiler_params=pltpu.CompilerParams(collective_id=0, has_side_effects=True, vmem_limit_bytes=54 * 1024 * 1024),
            name='outer_mean_ring',
        )(*[pltpu.with_memory_space_constraint(part, pltpu.HBM)
            for part in (z_rows, x, ln_scale, ln_offset, w_a.T, b_a, w_b.T, b_b, w_out, b_out)])
        made = [pltpu.with_memory_space_constraint(part, pltpu.VMEM) for part in made]
        return pl.pallas_call(
            functools.partial(last_kernel, n_dev),
            out_shape=jax.ShapeDtypeStruct(z_rows.shape, BF16),
            in_specs=[vmem_spec] * len(outs),
            out_specs=any_spec,
            scratch_shapes=[vmem((n_loc, 2 * HALF, pair), BF16), dma((n_dev,))],
            compiler_params=pltpu.CompilerParams(vmem_limit_bytes=8 * 1024 * 1024),
            name='outer_mean_last',
        )(*made)

    return jax.shard_map(local_update, mesh=mesh, in_specs=(row_spec, col_spec) + (rep_spec,) * 8, out_specs=row_spec, check_vma=False)
```

time: 51.7 us -> 46.8 us (0.905)
  local copies, waits for them, and re-layouts: 5.62 us -> 0 us
  Pallas kernels: 45.7 us -> 46.5 us
    unnamed x16 -> x0, local copies, waits for them, and re-layouts: 5.62 us -> none
    pallas_call x1, Pallas kernels: 43.5 us -> 44.6 us  [local_update(): pl.pallas_call(functools.partial(kernel, n_dev), out_shape=outs, in_specs...]
where the time goes in v3:
time: 46.8 us; the launch traced here: 46.7 us
  Pallas kernels  46.5 us (99%)
    pallas_call x1, Pallas kernels, local_update(): pl.pallas_call(functools.partial(kernel, n_dev), out_shape=outs, in_specs...  44.6 us
    pallas_call x1, Pallas kernels, local_update(): pl.pallas_call(functools.partial(last_kernel, n_dev), out_shape=jax.Shape...  1.95 us

profile of v3, /device:TPU:81, one launch (start us, length us, event | category | flops | bytes accessed | tf_op | source)
XLA Modules:
  0.0 46.7 jit_solution(16369681905745882361)
XLA Ops:
  0.0 44.6 %outer_mean_ring.1 = (bf16[32,256,128]{2,1,0:T(8,128)(2,1)S(1)}, bf16[512,1024]{1,0:T(8,128)(2,1)S(1)}, bf16[1024,512]{1,0:T(8,128)(2,1)S(1)}, f32[2,2,128,512]{...) custom-call(bf16[32,256,128]{2,1,0:T(8,128)(2,1)} %z_hbm.1, bf16[2048,512]{1,0:T(8,128)(2,1)} %bitcast.5, bf16[64]{0:T(256)(128)(2,1)} %ls_hbm.1, ...), custom_call_target="tpu_custom_call" | custom-call | tf_op jit(solution)/shard_map/outer_mean_ring/pallas_call | solution.py:375
  44.6 2.0 %outer_mean_last.1 = bf16[32,256,128]{2,1,0:T(8,128)(2,1)} custom-call(bf16[32,256,128]{2,1,0:T(8,128)(2,1)S(1)} %get-tuple-element.10.z_buf, bf16[512,1024]{1,0:T(8,128)(2,1)S(1)} %get-tuple-element.11.a_mat, bf16[1024,512]{1,0:T(8,128)(2,1)S(1)} %get-tuple-element.12.w_last, f32[2,2,128,512]{3,2,1,0:T(8,128)S(1)} %get-tuple-element.13.u_last, ...), custom_call_target="tpu_custom_call" | custom-call | tf_op jit(solution)/shard_map/outer_mean_last/pallas_call | solution.py:398

commit v4 on v3

--- a/solution.py
+++ b/solution.py
@@ -15,7 +15,7 @@
 PIECES = 4
 BLOCK = 128
 ALL = ('rows', 0, 4)
-FIRST_OWN = (('lanes', 0), ('lanes', 1))
+FIRST_OWN = (('lanes', 0, 128), ('lanes', 128, 256), ('lanes', 256, 512))
 SECOND_OWN = (('rows', 0, 2), ('rows', 2, 4))
 SHARED = (('rows', 0, 2), ('rows', 2, 3))
 FINAL = ('rows', 3, 4)
@@ -30,6 +30,15 @@
     spread = jnp.broadcast_to(row, (count, count))
     picked = jnp.where(iota((count, count), 0) == iota((count, count), 1), spread, 0.0)
     return jnp.broadcast_to(jnp.sum(picked, axis=1, keepdims=True), (count, LANES))
+
+
+def pair_product(lhs, a_mat, w_part, inv_seq):
+    res = jnp.dot(jnp.concatenate(lhs, axis=0), a_mat[...], preferred_element_type=F32)
+    res = (res * inv_seq).astype(BF16)
+    wide = jnp.concatenate(
+        [jnp.concatenate([res[h * BLOCK + d * HALF:h * BLOCK + (d + 1) * HALF, g * LANES:(g + 1) * LANES] for d in range(8)], axis=1)
+         for h in range(2) for g in range(8)], axis=0)
+    return jnp.dot(wide, w_part, preferred_element_type=F32)
 
 
 def kernel(n_dev, z_hbm, x_hbm, ls_hbm, lo_hbm, wa_hbm, ba_hbm, wb_hbm, bb_hbm, wo_hbm, bo_hbm,
@@ -57,11 +66,11 @@
         (wo_hbm, wo_v), (bo_hbm, bo_v)))]
     half_rows = HALF * m_dim
     half_seq = n_seq // 2
-    parts = [(slice(k * half_rows // 2, (k + 1) * half_rows // 2), slice(p * half_seq, (p + 1) * half_seq))
-             for p in range(2) for k in range(2)]
+    parts = [(slice(k * half_rows // 2, (k + 1) * half_rows // 2), slice(*group[1:]))
+             for group in FIRST_OWN for k in range(2)]
     parts += [(slice(half_rows + k * half_rows // 2, half_rows + (k + 1) * half_rows // 2), slice(0, n_seq)) for k in range(2)]
     x_copies = [pltpu.make_async_copy(x_hbm.at[part], x_buf.at[part], x_sem.at[k]) for k, part in enumerate(parts)]
-    for copy in x_copies[:2] + small[:4] + x_copies[2:4]:
+    for copy in small[:4] + x_copies[:6]:
         copy.start()
     z_copy = pltpu.make_async_copy(z_hbm, z_buf, z_sem)
 
@@ -72,14 +81,15 @@
     wb_two = jnp.concatenate([wb_rows, wb_rows], axis=1)
     scale_bc[...] = column_lanes(ls_v[...].astype(F32).reshape(1, m_dim), m_dim)
     offset_bc[...] = column_lanes(lo_v[...].astype(F32).reshape(1, m_dim), m_dim)
-    in_half = iota((HALF, LANES), 0)
-    in_pair = iota((HALF, LANES), 1) // m_dim
-    for d in range(hid):
-        spread = jnp.broadcast_to(wb_two[d:d + 1, :], (HALF, LANES))
-        for t in range(HALF * m_dim // LANES):
-            part = jnp.where(in_half == in_pair + 2 * t, spread, 0.0)
-            proj_b_w[d * HALF:(d + 1) * HALF, t * LANES:(t + 1) * LANES] = part.astype(BF16)
-        bias_b[d * HALF:(d + 1) * HALF, :] = jnp.broadcast_to(row_bc[d:d + 1, :], (HALF, LANES))
+    in_eight = iota((8, LANES), 0)
+    in_pair = iota((8, LANES), 1) // m_dim
+    for d in range(0, hid, 2):
+        for t in range(8 * m_dim // LANES):
+            part = [jnp.where(in_eight == in_pair + 2 * t, jnp.broadcast_to(wb_two[e:e + 1, :], (8, LANES)), 0.0)
+                    for e in (d, d + 1)]
+            proj_b_w[d * 8:(d + 2) * 8, t * LANES:(t + 1) * LANES] = jnp.concatenate(part, axis=0).astype(BF16)
+        for e in (d, d + 1):
+            bias_b[e * 8:(e + 1) * 8, :] = jnp.broadcast_to(row_bc[e:e + 1, :], (8, LANES))
 
     def norm_part(rows, lanes):
         width = lanes.stop - lanes.start
@@ -96,7 +106,7 @@
             x_buf[at] = (normed * scale + offset).astype(BF16)
             return carry
 
-        lax.fori_loop(0, (rows.stop - rows.start) // m_dim, body, 0, unroll=4)
+        lax.fori_loop(0, (rows.stop - rows.start) // m_dim, body, 0, unroll=8)
 
     def slot_of(q, r, h):
         return q * 8 + r * 2 + h
@@ -104,7 +114,8 @@
     def view(q, r, h, group):
         slot = slot_of(q, r, h)
         if group[0] == 'lanes':
-            return bt.at[slot, group[1]]
+            k = group[1] // half_seq
+            return bt.at[slot, k, :, pl.ds(group[1] - k * half_seq, group[2] - group[1])]
         if r == 2 and group == FINAL and q == 1:
             return bt_last.at[h]
         if group == ALL:
@@ -117,11 +128,11 @@
         if r_there == 2:
             k = SHARED.index(group) if group != FINAL else 2
         else:
-            k = 0 if group in (ALL, FIRST_OWN[0], SECOND_OWN[0]) else 1
+            k = 0 if group == ALL else (FIRST_OWN if group in FIRST_OWN else SECOND_OWN).index(group)
         k = sems.setdefault((r_there, h, k), len(sems))
         return pltpu.make_async_remote_copy(
             src_ref=view(q, r, h, group), dst_ref=view(q, r_there, h, group), send_sem=send_sem,
-            recv_sem=recv_sem.at[q * 16 + k], device_id={'dap': peer}, device_id_type=MESH)
+            recv_sem=recv_sem.at[q * 18 + k], device_id={'dap': peer}, device_id_type=MESH)
 
     def arrived(q, r, h, group):
         transfer(q, r, h, group, sib, r).wait_recv()
@@ -137,34 +148,36 @@
 
     own, other = core, 1 - core
 
-    def project_b(h, c, lanes):
-        rows = slice(c * BLOCK, (c + 1) * BLOCK)
+    def project_b(h, lanes):
         width = lanes.stop - lanes.start
-        res = jnp.dot(proj_b_w[rows, :], x_buf[h * half_rows:(h + 1) * half_rows, lanes], preferred_element_type=F32)
-        res = (res + jnp.concatenate([bias_b[rows, :]] * (width // LANES), axis=1)).astype(BF16)
-        for k in range(width // half_seq):
-            bt[slot_of(own, 0, h), lanes.start // half_seq + k, rows, :] = res[:, k * half_seq:(k + 1) * half_seq]
-
-    for p in range(2):
+        bias = jnp.concatenate([bias_b[...]] * (width // LANES), axis=1)
+        res = [jnp.dot(proj_b_w[...], x_buf[h * half_rows + k * half_rows // 2:h * half_rows + (k + 1) * half_rows // 2, lanes],
+                       preferred_element_type=F32) + bias for k in range(2)]
+        for d in range(hid):
+            rows = jnp.concatenate([part[d * 8:(d + 1) * 8, :] for part in res], axis=0).astype(BF16)
+            for at in range(lanes.start, lanes.stop, LANES):
+                k = at // half_seq
+                bt[slot_of(own, 0, h), k, d * HALF:(d + 1) * HALF, at - k * half_seq:at - k * half_seq + LANES] = (
+                    rows[:, at - lanes.start:at - lanes.start + LANES])
+
+    for p, group in enumerate(FIRST_OWN):
         for k in range(2):
             x_copies[2 * p + k].wait()
             norm_part(*parts[2 * p + k])
         if p == 0:
-            for copy in x_copies[4:] + small[4:] + [z_copy]:
+            for copy in x_copies[6:] + small[4:] + [z_copy]:
                 copy.start()
-        for c in range(PIECES):
-            project_b(0, c, parts[2 * p][1])
+        project_b(0, parts[2 * p][1])
         if p == 0:
             pl.semaphore_wait(barrier, 3)
-        to_right(own, 0, 0, FIRST_OWN[p])
-        to_left(own, 0, 0, FIRST_OWN[p])
+        to_right(own, 0, 0, group)
+        to_left(own, 0, 0, group)
     to_sib(own, 0, 0, ALL)
     for k in range(2):
-        x_copies[4 + k].wait()
-        norm_part(*parts[4 + k])
+        x_copies[6 + k].wait()
+        norm_part(*parts[6 + k])
+    project_b(1, parts[6][1])
     for group in SECOND_OWN:
-        for c in range(*group[1:]):
-            project_b(1, c, parts[4][1])
         to_right(own, 0, 1, group)
         to_left(own, 0, 1, group)
     to_sib(own, 0, 1, ALL)
@@ -248,7 +261,7 @@
         arrived(other, 0, h, ALL)
         half_unit(other, 0, h)
     for h in range(2):
-        for k, group in enumerate(FIRST_OWN if h == 0 else SECOND_OWN):
+        for k, group in enumerate(SECOND_OWN if h else FIRST_OWN):
             arrived(own, 3, h, group)
             arrived(own, 1, h, group)
             if h == 1:
@@ -274,26 +287,23 @@
         for r in (3, 1):
             half_unit(other, r, h)
 
-    def part_unit(q, h, group):
-        slot = slot_of(q, 2, h)
-        for c in range(*group[1:]):
-            outer_piece(slot, c)
-        update = project_piece(group[1])
-        for c in range(group[1] + 1, group[2]):
-            update = update + project_piece(c)
-        return update
-
-    wide_bias = jnp.concatenate([bias_out] * 4, axis=1)
-    for group in SHARED:
-        for h in range(2):
-            arrived(own, 2, h, group)
-            to_sib(own, 2, h, group)
-        for q in (own, other):
+    def pair_update(q, c):
+        rows = slice(c * BLOCK, (c + 1) * BLOCK)
+        lhs = [jnp.concatenate([bt[slot_of(q, 2, h), k, rows, :] for k in range(2)], axis=1) for h in range(2)]
+        return pair_product(lhs, a_mat, w_diag[c] if c < PIECES - 1 else w_last[...], inv_seq)
+
+    for h in range(2):
+        arrived(own, 2, h, SHARED[0])
+        to_sib(own, 2, h, SHARED[0])
+    for q in (own, other):
+        if q is other:
             for h in range(2):
-                if q is other:
-                    arrived(other, 2, h, group)
-                update = part_unit(q, h, group)
-                u_last[q, h] = update + wide_bias if group is SHARED[0] else u_last[q, h] + update
+                arrived(other, 2, h, SHARED[0])
+        u_last[q] = pair_update(q, 0) + pair_update(q, 1) + jnp.concatenate([bias_out] * 4, axis=1)
+    for h in range(2):
+        arrived(own, 2, h, SHARED[1])
+        to_sib(own, 2, h, SHARED[1])
+    u_last[own] = u_last[own] + pair_update(own, 2)
     for h in range(2):
         arrived(0, 2, h, FINAL)
 
@@ -302,13 +312,23 @@
             to_sib(0, 2, h, FINAL)
 
     for h in range(2):
-        finish(u_last[0, h] + part_unit(0, h, FINAL), None, 0, 2, h)
-    for h in range(2):
-        arrived(1, 2, h, FINAL)
-
-        @pl.when(core == 1)
-        def _():
+        arrived(other, 2, h, SHARED[1])
+    u_last[other] = u_last[other] + pair_update(other, 2)
+
+    @pl.when(core == 1)
+    def _():
+        for h in range(2):
+            arrived(1, 2, h, FINAL)
             to_sib(1, 2, h, FINAL)
+
+    update = u_last[0] + pair_update(0, PIECES - 1)
+    for h in range(2):
+        finish(update[h * BLOCK:(h + 1) * BLOCK, :], None, 0, 2, h)
+
+    @pl.when(core == 0)
+    def _():
+        for h in range(2):
+            arrived(1, 2, h, FINAL)
 
     for q, slots in enumerate((13, 15)):
         @pl.when(core == q)
@@ -331,20 +351,15 @@
     copies = [pltpu.make_async_copy(z_buf.at[:, block(k), :], out_hbm.at[:, block(k), :], sem.at[k]) for k in range(1, n_dev)]
     for copy in copies:
         copy.start()
-    lhs = jnp.concatenate([jnp.concatenate([bt_last[h, 0], bt_last[h, 1]], axis=1) for h in range(2)], axis=0)
-    res = jnp.dot(lhs, a_mat[...], preferred_element_type=F32)
-    res = (res * inv_seq).astype(BF16)
-    wide = jnp.concatenate(
-        [jnp.concatenate([res[h * BLOCK + d * HALF:h * BLOCK + (d + 1) * HALF, g * LANES:(g + 1) * LANES] for d in range(8)], axis=1)
-         for h in range(2) for g in range(8)], axis=0)
-    update = jnp.dot(wide, w_last[...], preferred_element_type=F32)
+    lhs = [jnp.concatenate([bt_last[h, 0], bt_last[h, 1]], axis=1) for h in range(2)]
+    update = u_last[1] + pair_product(lhs, a_mat, w_last[...], inv_seq)
     for h in range(2):
         cols = pl.ds(pl.multiple_of(mine * width + h * HALF, HALF), HALF)
         for g in range(8):
             for k in range(4):
                 i = g * 4 + k
-                rows, lanes = slice(g * HALF, (g + 1) * HALF), slice(k * LANES, (k + 1) * LANES)
-                part = u_last[1, h, rows, lanes] + update[h * BLOCK + g * HALF:h * BLOCK + (g + 1) * HALF, lanes]
+                lanes = slice(k * LANES, (k + 1) * LANES)
+                part = update[h * BLOCK + g * HALF:h * BLOCK + (g + 1) * HALF, lanes]
                 cols_buf[i, h * HALF:(h + 1) * HALF, :] = (z_buf[i, cols, :].astype(F32) + part).astype(BF16)
     copy = pltpu.make_async_copy(cols_buf, out_hbm.at[:, block(0), :], sem.at[0])
     copy.start()
@@ -369,7 +384,7 @@
         dma = pltpu.SemaphoreType.DMA
         outs = [
             vmem(z_rows.shape, BF16), vmem((n_seq, n_loc * hid), BF16), vmem((8 * LANES, 4 * pair), BF16),
-            vmem((2, 2, LANES, 4 * pair), F32), vmem((2, 2, BLOCK, n_seq // 2), BF16),
+            vmem((2, 2 * BLOCK, 4 * pair), F32), vmem((2, 2, BLOCK, n_seq // 2), BF16),
         ]
         vmem_spec = pl.BlockSpec(memory_space=pltpu.VMEM)
         made = pl.pallas_call(
@@ -383,12 +398,12 @@
                 vmem((hid, m_dim), BF16), vmem((hid,), BF16), vmem((hid, m_dim), BF16), vmem((hid,), BF16),
                 vmem(w_out.shape, BF16), vmem((pair,), BF16),
                 vmem((m_dim, LANES), F32), vmem((m_dim, LANES), F32),
-                vmem((4 * hid, LANES), F32), vmem((HALF * hid, LANES), F32), vmem((hid, LANES), F32),
-                vmem((4 * hid, 4 * m_dim), BF16), vmem((HALF * hid, HALF * m_dim), BF16),
+                vmem((4 * hid, LANES), F32), vmem((8 * hid, LANES), F32), vmem((hid, LANES), F32),
+                vmem((4 * hid, 4 * m_dim), BF16), vmem((8 * hid, 8 * m_dim), BF16),
                 vmem((16, 2, PIECES * BLOCK, n_seq // 2), BF16),
                 vmem((PIECES, LANES, 8 * LANES), BF16),
                 vmem(w_out.shape, F32), vmem((PIECES - 1, 8 * LANES, 4 * pair), BF16),
-                dma((8,)), dma((6,)), dma, dma((32,)), dma,
+                dma((8,)), dma((8,)), dma, dma((36,)), dma,
             ],
             compiler_params=pltpu.CompilerParams(collective_id=0, has_side_effects=True, vmem_limit_bytes=54 * 1024 * 1024),
             name='outer_mean_ring',

time: 46.8 us -> 44.6 us (0.953)
  Pallas kernels: 46.5 us -> 44.3 us
    pallas_call x1, Pallas kernels: 44.6 us -> 42.3 us  [local_update(): pl.pallas_call(functools.partial(kernel, n_dev), out_shape=outs, in_specs...]
where the time goes in v4:
time: 44.6 us; the launch traced here: 44.5 us
  Pallas kernels  44.3 us (99%)
    pallas_call x1, Pallas kernels, local_update(): pl.pallas_call(functools.partial(kernel, n_dev), out_shape=outs, in_specs...  42.3 us
    pallas_call x1, Pallas kernels, local_update(): pl.pallas_call(functools.partial(last_kernel, n_dev), out_shape=jax.Shape...  1.95 us

profile of v4, /device:TPU:81, one launch (start us, length us, event | category | flops | bytes accessed | tf_op | source)
XLA Modules:
  0.0 44.5 jit_solution(5454941699394147475)
XLA Ops:
  0.0 42.3 %outer_mean_ring.1 = (bf16[32,256,128]{2,1,0:T(8,128)(2,1)S(1)}, bf16[512,1024]{1,0:T(8,128)(2,1)S(1)}, bf16[1024,512]{1,0:T(8,128)(2,1)S(1)}, f32[2,256,512]{2,1,0:T(8,128)S(1)}, bf16[2,2,128,256]{3,2,1,0:T(8,128)(2,1)S(1)}) custom-call(bf16[32,256,128]{2,1,0:T(8,128)(2,1)} %z_hbm.1, bf16[2048,512]{1,0:T(8,128)(2,1)} %bitcast.5, bf16[64]{0:T(256)(128)(2,1)} %ls_hbm.1, ...), custom_call_target="tpu_custom_call" | custom-call | tf_op jit(solution)/shard_map/outer_mean_ring/pallas_call | solution.py:390
  42.4 1.9 %outer_mean_last.1 = bf16[32,256,128]{2,1,0:T(8,128)(2,1)} custom-call(bf16[32,256,128]{2,1,0:T(8,128)(2,1)S(1)} %get-tuple-element.10.z_buf, bf16[512,1024]{1,0:T(8,128)(2,1)S(1)} %get-tuple-element.11.a_mat, bf16[1024,512]{1,0:T(8,128)(2,1)S(1)} %get-tuple-element.12.w_last, f32[2,256,512]{2,1,0:T(8,128)S(1)} %get-tuple-element.13.u_last, ...), custom_call_target="tpu_custom_call" | custom-call | tf_op jit(solution)/shard_map/outer_mean_last/pallas_call | solution.py:413

commit v5 on v4

--- a/solution.py
+++ b/solution.py
@@ -19,6 +19,7 @@
 SECOND_OWN = (('rows', 0, 2), ('rows', 2, 4))
 SHARED = (('rows', 0, 2), ('rows', 2, 3))
 FINAL = ('rows', 3, 4)
+CLOSING = (('rows', 3, 3.5), ('rows', 3.5, 4))
 MESH = pl.DeviceIdType.MESH
 
 
@@ -35,8 +36,9 @@
 def pair_product(lhs, a_mat, w_part, inv_seq):
     res = jnp.dot(jnp.concatenate(lhs, axis=0), a_mat[...], preferred_element_type=F32)
     res = (res * inv_seq).astype(BF16)
+    size = lhs[0].shape[0]
     wide = jnp.concatenate(
-        [jnp.concatenate([res[h * BLOCK + d * HALF:h * BLOCK + (d + 1) * HALF, g * LANES:(g + 1) * LANES] for d in range(8)], axis=1)
+        [jnp.concatenate([res[at:at + HALF, g * LANES:(g + 1) * LANES] for at in range(h * size, (h + 1) * size, HALF)], axis=1)
          for h in range(2) for g in range(8)], axis=0)
     return jnp.dot(wide, w_part, preferred_element_type=F32)
 
@@ -116,35 +118,49 @@
         if group[0] == 'lanes':
             k = group[1] // half_seq
             return bt.at[slot, k, :, pl.ds(group[1] - k * half_seq, group[2] - group[1])]
-        if r == 2 and group == FINAL and q == 1:
-            return bt_last.at[h]
         if group == ALL:
             return bt.at[slot]
-        return bt.at[slot, :, pl.ds(group[1] * BLOCK, (group[2] - group[1]) * BLOCK), :]
-
-    sems = {}
-
-    def transfer(q, r, h, group, peer, r_there):
-        if r_there == 2:
-            k = SHARED.index(group) if group != FINAL else 2
+        return bt.at[slot, :, pl.ds(int(group[1] * BLOCK), int((group[2] - group[1]) * BLOCK)), :]
+
+    names = ['own first', 'own second r3', 'own second r1 0', 'own second r1 1', 'own shared 0', 'own shared 1', 'other r0',
+             'other first', 'other second', 'other shared 0', 'other shared 1', 'final', 'closing 0', 'closing 1']
+
+    def semaphore_name(mine, r, h, group):
+        if group == FINAL:
+            return 'final'
+        if group in CLOSING:
+            return f'closing {CLOSING.index(group)}'
+        if r == 2:
+            return ('own' if mine else 'other') + f' shared {SHARED.index(group)}'
+        if not mine:
+            return 'other r0' if r == 0 else 'other second' if h else 'other first'
+        if h == 0:
+            return 'own first'
+        return 'own second r3' if r == 3 else f'own second r1 {SECOND_OWN.index(group)}'
+
+    def transfer(src, dst, name, peer):
+        return pltpu.make_async_remote_copy(
+            src_ref=src, dst_ref=dst, send_sem=send_sem, recv_sem=recv_sem.at[names.index(name)], device_id={'dap': peer},
+            device_id_type=MESH)
+
+    def arrived(name, halves):
+        if halves >= 1:
+            shape = bt.at[pl.ds(0, halves)]
         else:
-            k = 0 if group == ALL else (FIRST_OWN if group in FIRST_OWN else SECOND_OWN).index(group)
-        k = sems.setdefault((r_there, h, k), len(sems))
-        return pltpu.make_async_remote_copy(
-            src_ref=view(q, r, h, group), dst_ref=view(q, r_there, h, group), send_sem=send_sem,
-            recv_sem=recv_sem.at[q * 18 + k], device_id={'dap': peer}, device_id_type=MESH)
-
-    def arrived(q, r, h, group):
-        transfer(q, r, h, group, sib, r).wait_recv()
-
-    def to_right(q, r, h, group):
-        transfer(q, r, h, group, right, (r + 3) % 4).start()
-
-    def to_left(q, r, h, group):
-        transfer(q, r, h, group, left, (r + 1) % 4).start()
+            shape = bt.at[pl.ds(0, 2), :, pl.ds(0, int(halves * PIECES * BLOCK) // 2)]
+        transfer(shape, shape, name, sib).wait_recv()
+
+    def to_right(q, r, h, group, mine=True):
+        there = (r + 3) % 4
+        transfer(view(q, r, h, group), view(q, there, h, group), semaphore_name(mine, there, h, group), right).start()
+
+    def to_left(q, r, h, group, mine=True):
+        there = (r + 1) % 4
+        transfer(view(q, r, h, group), view(q, there, h, group), semaphore_name(mine, there, h, group), left).start()
 
     def to_sib(q, r, h, group):
-        transfer(q, r, h, group, sib, r).start()
+        dst = bt_last.at[h] if group == CLOSING[1] else view(q, r, h, group)
+        transfer(view(q, r, h, group), dst, semaphore_name(False, r, h, group), sib).start()
 
     own, other = core, 1 - core
 
@@ -257,78 +273,86 @@
     z_copy.wait()
     for h in range(2):
         half_unit(own, 0, h)
+    arrived('other r0', 2)
     for h in range(2):
-        arrived(other, 0, h, ALL)
         half_unit(other, 0, h)
     for h in range(2):
-        for k, group in enumerate(SECOND_OWN if h else FIRST_OWN):
-            arrived(own, 3, h, group)
-            arrived(own, 1, h, group)
-            if h == 1:
-                to_left(own, 1, 1, SHARED[k])
         if h == 0:
+            arrived('own first', 2)
             for group in SHARED:
                 to_right(own, 3, 0, group)
+        else:
+            for k in range(2):
+                arrived(f'own second r1 {k}', 0.5)
+                to_left(own, 1, 1, SHARED[k])
+            arrived('own second r3', 1)
         for r in (3, 1):
             to_sib(own, r, h, ALL)
         for r in (3, 1):
             half_unit(own, r, h)
-        for r in (3, 1):
-            arrived(other, r, h, ALL)
+        arrived('other second' if h else 'other first', 2)
 
         @pl.when(core == 1)
         def _():
-            for q in range(2):
-                if h == 0:
-                    to_right(q, 3, 0, FINAL)
-                else:
-                    to_left(q, 1, 1, FINAL)
+            for q, groups in ((0, (FINAL,)), (1, CLOSING)):
+                for group in groups:
+                    if h == 0:
+                        to_right(q, 3, 0, group)
+                    else:
+                        to_left(q, 1, 1, group)
 
         for r in (3, 1):
             half_unit(other, r, h)
 
-    def pair_update(q, c):
-        rows = slice(c * BLOCK, (c + 1) * BLOCK)
+    def pair_update(q, group):
+        rows = slice(int(group[1] * BLOCK), int(group[2] * BLOCK))
         lhs = [jnp.concatenate([bt[slot_of(q, 2, h), k, rows, :] for k in range(2)], axis=1) for h in range(2)]
-        return pair_product(lhs, a_mat, w_diag[c] if c < PIECES - 1 else w_last[...], inv_seq)
-
+        c = int(group[1])
+        at = slice(int((group[1] - c) * 8 * LANES), int((group[2] - c) * 8 * LANES))
+        return pair_product(lhs, a_mat, w_diag[c, at, :] if c < PIECES - 1 else w_last[at, :], inv_seq)
+
+    def finish_pair(update, q):
+        for h in range(2):
+            finish(update[h * BLOCK:(h + 1) * BLOCK, :], None, q, 2, h)
+
+    first_pieces = (('rows', 0, 1), ('rows', 1, 2))
+    for q in (own, other):
+        arrived('own shared 0' if q is own else 'other shared 0', 1)
+        if q is own:
+            for h in range(2):
+                to_sib(own, 2, h, SHARED[0])
+        u_last[q] = pair_update(q, first_pieces[0]) + pair_update(q, first_pieces[1]) + jnp.concatenate([bias_out] * 4, axis=1)
+    arrived('own shared 1', 0.5)
     for h in range(2):
-        arrived(own, 2, h, SHARED[0])
-        to_sib(own, 2, h, SHARED[0])
-    for q in (own, other):
-        if q is other:
-            for h in range(2):
-                arrived(other, 2, h, SHARED[0])
-        u_last[q] = pair_update(q, 0) + pair_update(q, 1) + jnp.concatenate([bias_out] * 4, axis=1)
-    for h in range(2):
-        arrived(own, 2, h, SHARED[1])
         to_sib(own, 2, h, SHARED[1])
-    u_last[own] = u_last[own] + pair_update(own, 2)
-    for h in range(2):
-        arrived(0, 2, h, FINAL)
-
-        @pl.when(core == 1)
-        def _():
-            to_sib(0, 2, h, FINAL)
-
-    for h in range(2):
-        arrived(other, 2, h, SHARED[1])
-    u_last[other] = u_last[other] + pair_update(other, 2)
+    u_last[own] = u_last[own] + pair_update(own, SHARED[1])
 
     @pl.when(core == 1)
     def _():
+        arrived('final', 0.5)
         for h in range(2):
-            arrived(1, 2, h, FINAL)
-            to_sib(1, 2, h, FINAL)
-
-    update = u_last[0] + pair_update(0, PIECES - 1)
-    for h in range(2):
-        finish(update[h * BLOCK:(h + 1) * BLOCK, :], None, 0, 2, h)
+            to_sib(0, 2, h, FINAL)
+        u_last[0] = u_last[0] + pair_update(0, FINAL)
+        arrived('closing 0', 0.25)
+        for h in range(2):
+            to_sib(1, 2, h, CLOSING[0])
+        arrived('other shared 1', 0.5)
+        u_last[0] = u_last[0] + pair_update(0, SHARED[1])
+        arrived('closing 1', 0.25)
+        for h in range(2):
+            to_sib(1, 2, h, CLOSING[1])
+        finish_pair(u_last[0], 0)
+        finish_pair(u_last[1] + pair_update(1, FINAL), 1)
 
     @pl.when(core == 0)
     def _():
-        for h in range(2):
-            arrived(1, 2, h, FINAL)
+        arrived('other shared 1', 0.5)
+        u_last[1] = u_last[1] + pair_update(1, SHARED[1])
+        arrived('final', 0.5)
+        finish_pair(u_last[0] + pair_update(0, FINAL), 0)
+        arrived('closing 0', 0.25)
+        u_last[1] = u_last[1] + pair_update(1, CLOSING[0])
+        arrived('closing 1', 0.25)
 
     for q, slots in enumerate((13, 15)):
         @pl.when(core == q)
@@ -348,22 +372,29 @@
     def block(k):
         return pl.ds(pl.multiple_of(lax.rem(mine + k, n_dev) * width, width), width)
 
-    copies = [pltpu.make_async_copy(z_buf.at[:, block(k), :], out_hbm.at[:, block(k), :], sem.at[k]) for k in range(1, n_dev)]
-    for copy in copies:
+    core = lax.rem(me, 2)
+    copies = [pltpu.make_async_copy(z_buf.at[:, block(k), :], out_hbm.at[:, block(k), :], sem.at[k]) for k in range(n_dev)]
+    for copy in copies[1:]:
         copy.start()
-    lhs = [jnp.concatenate([bt_last[h, 0], bt_last[h, 1]], axis=1) for h in range(2)]
-    update = u_last[1] + pair_product(lhs, a_mat, w_last[...], inv_seq)
-    for h in range(2):
-        cols = pl.ds(pl.multiple_of(mine * width + h * HALF, HALF), HALF)
-        for g in range(8):
-            for k in range(4):
-                i = g * 4 + k
-                lanes = slice(k * LANES, (k + 1) * LANES)
-                part = update[h * BLOCK + g * HALF:h * BLOCK + (g + 1) * HALF, lanes]
-                cols_buf[i, h * HALF:(h + 1) * HALF, :] = (z_buf[i, cols, :].astype(F32) + part).astype(BF16)
-    copy = pltpu.make_async_copy(cols_buf, out_hbm.at[:, block(0), :], sem.at[0])
-    copy.start()
-    copies.append(copy)
+
+    @pl.when(core == 1)
+    def _():
+        copies[0].start()
+
+    @pl.when(core == 0)
+    def _():
+        lhs = [jnp.concatenate([bt_last[h, 0], bt_last[h, 1]], axis=1) for h in range(2)]
+        rows = lhs[0].shape[0] * 8
+        update = u_last[1] + pair_product(lhs, a_mat, w_last[w_last.shape[0] - rows:, :], inv_seq)
+        for h in range(2):
+            cols = pl.ds(pl.multiple_of(mine * width + h * HALF, HALF), HALF)
+            for g in range(8):
+                for k in range(4):
+                    i = g * 4 + k
+                    part = update[h * BLOCK + g * HALF:h * BLOCK + (g + 1) * HALF, k * LANES:(k + 1) * LANES]
+                    cols_buf[i, h * HALF:(h + 1) * HALF, :] = (z_buf[i, cols, :].astype(F32) + part).astype(BF16)
+        pltpu.make_async_copy(cols_buf, out_hbm.at[:, block(0), :], sem.at[0]).start()
+
     for copy in copies:
         copy.wait()
 
@@ -384,7 +415,7 @@
         dma = pltpu.SemaphoreType.DMA
         outs = [
             vmem(z_rows.shape, BF16), vmem((n_seq, n_loc * hid), BF16), vmem((8 * LANES, 4 * pair), BF16),
-            vmem((2, 2 * BLOCK, 4 * pair), F32), vmem((2, 2, BLOCK, n_seq // 2), BF16),
+            vmem((2, 2 * BLOCK, 4 * pair), F32), vmem((2, 2, BLOCK // 2, n_seq // 2), BF16),
         ]
         vmem_spec = pl.BlockSpec(memory_space=pltpu.VMEM)
         made = pl.pallas_call(
@@ -403,7 +434,7 @@
                 vmem((16, 2, PIECES * BLOCK, n_seq // 2), BF16),
                 vmem((PIECES, LANES, 8 * LANES), BF16),
                 vmem(w_out.shape, F32), vmem((PIECES - 1, 8 * LANES, 4 * pair), BF16),
-                dma((8,)), dma((8,)), dma, dma((36,)), dma,
+                dma((8,)), dma((8,)), dma, dma((14,)), dma,
             ],
             compiler_params=pltpu.CompilerParams(collective_id=0, has_side_effects=True, vmem_limit_bytes=54 * 1024 * 1024),
             name='outer_mean_ring',

time: 44.6 us -> 44 us (0.987)
  Pallas kernels: 44.3 us -> 43.8 us
    pallas_call x1, Pallas kernels: 1.95 us -> 1.41 us  [local_update(): pl.pallas_call(functools.partial(last_kernel, n_dev), out_shape=jax.Shape...]
where the time goes in v5:
time: 44 us
  Pallas kernels  43.8 us (100%)
    pallas_call x1, Pallas kernels, local_update(): pl.pallas_call(functools.partial(kernel, n_dev), out_shape=outs, in_specs...  42.4 us
    pallas_call x1, Pallas kernels, local_update(): pl.pallas_call(functools.partial(last_kernel, n_dev), out_shape=jax.Shape...  1.41 us

profile of v5, /device:TPU:81, one launch (start us, length us, event | category | flops | bytes accessed | tf_op | source)
XLA Modules:
  0.0 44.0 jit_solution(1080339586706244700)
XLA Ops:
  0.0 42.4 %outer_mean_ring.1 = (bf16[32,256,128]{2,1,0:T(8,128)(2,1)S(1)}, bf16[512,1024]{1,0:T(8,128)(2,1)S(1)}, bf16[1024,512]{1,0:T(8,128)(2,1)S(1)}, f32[2,256,512]{2,1,0:T(8,128)S(1)}, bf16[2,2,64,256]{3,2,1,0:T(8,128)(2,1)S(1)}) custom-call(bf16[32,256,128]{2,1,0:T(8,128)(2,1)} %z_hbm.1, bf16[2048,512]{1,0:T(8,128)(2,1)} %bitcast.5, bf16[64]{0:T(256)(128)(2,1)} %ls_hbm.1, ...), custom_call_target="tpu_custom_call" | custom-call | tf_op jit(solution)/shard_map/outer_mean_ring/pallas_call | solution.py:421
  42.4 1.4 %outer_mean_last.1 = bf16[32,256,128]{2,1,0:T(8,128)(2,1)} custom-call(bf16[32,256,128]{2,1,0:T(8,128)(2,1)S(1)} %get-tuple-element.10.z_buf, bf16[512,1024]{1,0:T(8,128)(2,1)S(1)} %get-tuple-element.11.a_mat, bf16[1024,512]{1,0:T(8,128)(2,1)S(1)} %get-tuple-element.12.w_last, f32[2,256,512]{2,1,0:T(8,128)S(1)} %get-tuple-element.13.u_last, ...), custom_call_target="tpu_custom_call" | custom-call | tf_op jit(solution)/shard_map/outer_mean_last/pallas_call | solution.py:444

commit v6 on v5

--- a/solution.py
+++ b/solution.py
@@ -17,7 +17,7 @@
 ALL = ('rows', 0, 4)
 FIRST_OWN = (('lanes', 0, 128), ('lanes', 128, 256), ('lanes', 256, 512))
 SECOND_OWN = (('rows', 0, 2), ('rows', 2, 4))
-SHARED = (('rows', 0, 2), ('rows', 2, 3))
+SHARED = (('rows', 0, 1), ('rows', 1, 2), ('rows', 2, 3))
 FINAL = ('rows', 3, 4)
 CLOSING = (('rows', 3, 3.5), ('rows', 3.5, 4))
 MESH = pl.DeviceIdType.MESH
@@ -122,8 +122,8 @@
             return bt.at[slot]
         return bt.at[slot, :, pl.ds(int(group[1] * BLOCK), int((group[2] - group[1]) * BLOCK)), :]
 
-    names = ['own first', 'own second r3', 'own second r1 0', 'own second r1 1', 'own shared 0', 'own shared 1', 'other r0',
-             'other first', 'other second', 'other shared 0', 'other shared 1', 'final', 'closing 0', 'closing 1']
+    names = ['own first', 'own second 0', 'own second 1', 'own shared 0', 'own shared 1', 'own shared 2', 'other r0',
+             'other first', 'other second 0', 'other second 1', 'other shared 0', 'other shared 1', 'other shared 2', 'final', 'closing 0', 'closing 1']
 
     def semaphore_name(mine, r, h, group):
         if group == FINAL:
@@ -133,10 +133,10 @@
         if r == 2:
             return ('own' if mine else 'other') + f' shared {SHARED.index(group)}'
         if not mine:
-            return 'other r0' if r == 0 else 'other second' if h else 'other first'
-        if h == 0:
-            return 'own first'
-        return 'own second r3' if r == 3 else f'own second r1 {SECOND_OWN.index(group)}'
+            if r == 0:
+                return 'other r0'
+            return f'other second {SECOND_OWN.index(group)}' if h else 'other first'
+        return f'own second {SECOND_OWN.index(group)}' if h else 'own first'
 
     def transfer(src, dst, name, peer):
         return pltpu.make_async_remote_copy(
@@ -276,22 +276,21 @@
     arrived('other r0', 2)
     for h in range(2):
         half_unit(other, 0, h)
-    for h in range(2):
-        if h == 0:
-            arrived('own first', 2)
-            for group in SHARED:
-                to_right(own, 3, 0, group)
-        else:
-            for k in range(2):
-                arrived(f'own second r1 {k}', 0.5)
-                to_left(own, 1, 1, SHARED[k])
-            arrived('own second r3', 1)
-        for r in (3, 1):
-            to_sib(own, r, h, ALL)
-        for r in (3, 1):
-            half_unit(own, r, h)
-        arrived('other second' if h else 'other first', 2)
-
+    def pair_update(q, slots, group):
+        rows = slice(int(group[1] * BLOCK), int(group[2] * BLOCK))
+        lhs = [jnp.concatenate([bt[slot_of(q, r, h), k, rows, :] for k in range(2)], axis=1) for r, h in slots]
+        c = int(group[1])
+        at = slice(int((group[1] - c) * 8 * LANES), int((group[2] - c) * 8 * LANES))
+        return pair_product(lhs, a_mat, w_diag[c, at, :] if c < PIECES - 1 else w_last[at, :], inv_seq)
+
+    def finish_pair(update, q, slots):
+        for k, (r, h) in enumerate(slots):
+            finish(update[k * BLOCK:(k + 1) * BLOCK, :], None, q, r, h)
+
+    far, near = ((2, 0), (2, 1)), ((3, 1), (1, 1))
+    wide_bias = jnp.concatenate([bias_out] * 4, axis=1)
+
+    def send_final(h):
         @pl.when(core == 1)
         def _():
             for q, groups in ((0, (FINAL,)), (1, CLOSING)):
@@ -301,57 +300,72 @@
                     else:
                         to_left(q, 1, 1, group)
 
+
+    arrived('own first', 2)
+    for group in SHARED:
+        to_right(own, 3, 0, group)
+    for r in (3, 1):
+        to_sib(own, r, 0, ALL)
+    for r in (3, 1):
+        half_unit(own, r, 0)
+    arrived('other first', 2)
+    send_final(0)
+    for r in (3, 1):
+        half_unit(other, r, 0)
+    for k, group in enumerate(SECOND_OWN):
+        arrived(f'own second {k}', 1)
+        for part in SHARED:
+            if group[1] <= part[1] < group[2]:
+                to_left(own, 1, 1, part)
         for r in (3, 1):
-            half_unit(other, r, h)
-
-    def pair_update(q, group):
-        rows = slice(int(group[1] * BLOCK), int(group[2] * BLOCK))
-        lhs = [jnp.concatenate([bt[slot_of(q, 2, h), k, rows, :] for k in range(2)], axis=1) for h in range(2)]
-        c = int(group[1])
-        at = slice(int((group[1] - c) * 8 * LANES), int((group[2] - c) * 8 * LANES))
-        return pair_product(lhs, a_mat, w_diag[c, at, :] if c < PIECES - 1 else w_last[at, :], inv_seq)
-
-    def finish_pair(update, q):
+            to_sib(own, r, 1, group)
+        blocks = [('rows', c, c + 1) for c in range(*group[1:])]
+        for q in (own, other):
+            if q is other:
+                arrived(f'other second {k}', 1)
+                if k == 1:
+                    send_final(1)
+            update = pair_update(q, near, blocks[0]) + pair_update(q, near, blocks[1])
+            if k == 0:
+                u_last[q] = update + wide_bias
+            else:
+                finish_pair(u_last[q] + update, q, near)
+
+    for k, group in enumerate(SHARED):
+        arrived(f'own shared {k}', 0.5)
         for h in range(2):
-            finish(update[h * BLOCK:(h + 1) * BLOCK, :], None, q, 2, h)
-
-    first_pieces = (('rows', 0, 1), ('rows', 1, 2))
-    for q in (own, other):
-        arrived('own shared 0' if q is own else 'other shared 0', 1)
-        if q is own:
-            for h in range(2):
-                to_sib(own, 2, h, SHARED[0])
-        u_last[q] = pair_update(q, first_pieces[0]) + pair_update(q, first_pieces[1]) + jnp.concatenate([bias_out] * 4, axis=1)
-    arrived('own shared 1', 0.5)
-    for h in range(2):
-        to_sib(own, 2, h, SHARED[1])
-    u_last[own] = u_last[own] + pair_update(own, SHARED[1])
+            to_sib(own, 2, h, group)
+        for q in (own, other)[:2 if k < 2 else 1]:
+            if q is other:
+                arrived(f'other shared {k}', 0.5)
+            update = pair_update(q, far, group)
+            u_last[q] = u_last[q] + update if k else update + wide_bias
 
     @pl.when(core == 1)
     def _():
         arrived('final', 0.5)
         for h in range(2):
             to_sib(0, 2, h, FINAL)
-        u_last[0] = u_last[0] + pair_update(0, FINAL)
+        u_last[0] = u_last[0] + pair_update(0, far, FINAL)
         arrived('closing 0', 0.25)
         for h in range(2):
             to_sib(1, 2, h, CLOSING[0])
-        arrived('other shared 1', 0.5)
-        u_last[0] = u_last[0] + pair_update(0, SHARED[1])
+        arrived('other shared 2', 0.5)
+        u_last[0] = u_last[0] + pair_update(0, far, SHARED[2])
         arrived('closing 1', 0.25)
         for h in range(2):
             to_sib(1, 2, h, CLOSING[1])
-        finish_pair(u_last[0], 0)
-        finish_pair(u_last[1] + pair_update(1, FINAL), 1)
+        finish_pair(u_last[0], 0, far)
+        finish_pair(u_last[1] + pair_update(1, far, FINAL), 1, far)
 
     @pl.when(core == 0)
     def _():
-        arrived('other shared 1', 0.5)
-        u_last[1] = u_last[1] + pair_update(1, SHARED[1])
+        arrived('other shared 2', 0.5)
+        u_last[1] = u_last[1] + pair_update(1, far, SHARED[2])
         arrived('final', 0.5)
-        finish_pair(u_last[0] + pair_update(0, FINAL), 0)
+        finish_pair(u_last[0] + pair_update(0, far, FINAL), 0, far)
         arrived('closing 0', 0.25)
-        u_last[1] = u_last[1] + pair_update(1, CLOSING[0])
+        u_last[1] = u_last[1] + pair_update(1, far, CLOSING[0])
         arrived('closing 1', 0.25)
 
     for q, slots in enumerate((13, 15)):
@@ -434,7 +448,7 @@
                 vmem((16, 2, PIECES * BLOCK, n_seq // 2), BF16),
                 vmem((PIECES, LANES, 8 * LANES), BF16),
                 vmem(w_out.shape, F32), vmem((PIECES - 1, 8 * LANES, 4 * pair), BF16),
-                dma((8,)), dma((8,)), dma, dma((14,)), dma,
+                dma((8,)), dma((8,)), dma, dma((17,)), dma,
             ],
             compiler_params=pltpu.CompilerParams(collective_id=0, has_side_effects=True, vmem_limit_bytes=54 * 1024 * 1024),
             name='outer_mean_ring',

time: 44 us -> 43.6 us (level)
  Pallas kernels: 43.8 us -> 43.3 us
    pallas_call x1, Pallas kernels: 42.4 us -> 41.9 us  [local_update(): pl.pallas_call(functools.partial(kernel, n_dev), out_shape=outs, in_specs...]
where the time goes in v6:
time: 43.6 us; the launch traced here: 43.5 us
  Pallas kernels  43.3 us (99%)
    pallas_call x1, Pallas kernels, local_update(): pl.pallas_call(functools.partial(kernel, n_dev), out_shape=outs, in_specs...  41.9 us
    pallas_call x1, Pallas kernels, local_update(): pl.pallas_call(functools.partial(last_kernel, n_dev), out_shape=jax.Shape...  1.41 us

profile of v6, /device:TPU:81, one launch (start us, length us, event | category | flops | bytes accessed | tf_op | source)
XLA Modules:
  0.0 43.5 jit_solution(3803710270546391089)
XLA Ops:
  0.0 41.9 %outer_mean_ring.1 = (bf16[32,256,128]{2,1,0:T(8,128)(2,1)S(1)}, bf16[512,1024]{1,0:T(8,128)(2,1)S(1)}, bf16[1024,512]{1,0:T(8,128)(2,1)S(1)}, f32[2,256,512]{2,1,0:T(8,128)S(1)}, bf16[2,2,64,256]{3,2,1,0:T(8,128)(2,1)S(1)}) custom-call(bf16[32,256,128]{2,1,0:T(8,128)(2,1)} %z_hbm.1, bf16[2048,512]{1,0:T(8,128)(2,1)} %bitcast.5, bf16[64]{0:T(256)(128)(2,1)} %ls_hbm.1, ...), custom_call_target="tpu_custom_call" | custom-call | tf_op jit(solution)/shard_map/outer_mean_ring/pallas_call | solution.py:435
  41.9 1.4 %outer_mean_last.1 = bf16[32,256,128]{2,1,0:T(8,128)(2,1)} custom-call(bf16[32,256,128]{2,1,0:T(8,128)(2,1)S(1)} %get-tuple-element.10.z_buf, bf16[512,1024]{1,0:T(8,128)(2,1)S(1)} %get-tuple-element.11.a_mat, bf16[1024,512]{1,0:T(8,128)(2,1)S(1)} %get-tuple-element.12.w_last, f32[2,256,512]{2,1,0:T(8,128)S(1)} %get-tuple-element.13.u_last, ...), custom_call_target="tpu_custom_call" | custom-call | tf_op jit(solution)/shard_map/outer_mean_last/pallas_call | solution.py:458

commit v7 on v6

--- a/solution.py
+++ b/solution.py
@@ -19,7 +19,7 @@
 SECOND_OWN = (('rows', 0, 2), ('rows', 2, 4))
 SHARED = (('rows', 0, 1), ('rows', 1, 2), ('rows', 2, 3))
 FINAL = ('rows', 3, 4)
-CLOSING = (('rows', 3, 3.5), ('rows', 3.5, 4))
+CLOSING = (('rows', 3, 3.75), ('rows', 3.75, 4))
 MESH = pl.DeviceIdType.MESH
 
 
@@ -76,6 +76,8 @@
         copy.start()
     z_copy = pltpu.make_async_copy(z_hbm, z_buf, z_sem)
 
+    for copy in x_copies[:2]:
+        copy.wait()
     for copy in small[:4]:
         copy.wait()
     row_bc[...] = column_lanes(bb_v[...].astype(F32).reshape(1, hid), hid)
@@ -93,13 +95,13 @@
         for e in (d, d + 1):
             bias_b[e * 8:(e + 1) * 8, :] = jnp.broadcast_to(row_bc[e:e + 1, :], (8, LANES))
 
-    def norm_part(rows, lanes):
+    def norm_part(rows, lanes, unrolled=False):
         width = lanes.stop - lanes.start
         scale = jnp.concatenate([scale_bc[...]] * (width // LANES), axis=1)
         offset = jnp.concatenate([offset_bc[...]] * (width // LANES), axis=1)
 
         def body(n, carry):
-            at = (pl.ds(pl.multiple_of(rows.start + n * m_dim, m_dim), m_dim), lanes)
+            at = (pl.ds(rows.start + n * m_dim if unrolled else pl.multiple_of(rows.start + n * m_dim, m_dim), m_dim), lanes)
             value = x_buf[at].astype(F32)
             mean = jnp.sum(value, axis=0, keepdims=True) * (1.0 / m_dim)
             centred = value - mean
@@ -108,7 +110,11 @@
             x_buf[at] = (normed * scale + offset).astype(BF16)
             return carry
 
-        lax.fori_loop(0, (rows.stop - rows.start) // m_dim, body, 0, unroll=8)
+        if unrolled:
+            for n in range((rows.stop - rows.start) // m_dim):
+                body(n, 0)
+        else:
+            lax.fori_loop(0, (rows.stop - rows.start) // m_dim, body, 0, unroll=8)
 
     def slot_of(q, r, h):
         return q * 8 + r * 2 + h
@@ -178,9 +184,10 @@
 
     for p, group in enumerate(FIRST_OWN):
         for k in range(2):
-            x_copies[2 * p + k].wait()
-            norm_part(*parts[2 * p + k])
-        if p == 0:
+            if p > 0:
+                x_copies[2 * p + k].wait()
+            norm_part(*parts[2 * p + k], unrolled=p == 0)
+        if p == 1:
             for copy in x_copies[6:] + small[4:] + [z_copy]:
                 copy.start()
         project_b(0, parts[2 * p][1])
@@ -347,12 +354,12 @@
         for h in range(2):
             to_sib(0, 2, h, FINAL)
         u_last[0] = u_last[0] + pair_update(0, far, FINAL)
-        arrived('closing 0', 0.25)
+        arrived('closing 0', 0.375)
         for h in range(2):
             to_sib(1, 2, h, CLOSING[0])
         arrived('other shared 2', 0.5)
         u_last[0] = u_last[0] + pair_update(0, far, SHARED[2])
-        arrived('closing 1', 0.25)
+        arrived('closing 1', 0.125)
         for h in range(2):
             to_sib(1, 2, h, CLOSING[1])
         finish_pair(u_last[0], 0, far)
@@ -364,9 +371,9 @@
         u_last[1] = u_last[1] + pair_update(1, far, SHARED[2])
         arrived('final', 0.5)
         finish_pair(u_last[0] + pair_update(0, far, FINAL), 0, far)
-        arrived('closing 0', 0.25)
+        arrived('closing 0', 0.375)
         u_last[1] = u_last[1] + pair_update(1, far, CLOSING[0])
-        arrived('closing 1', 0.25)
+        arrived('closing 1', 0.125)
 
     for q, slots in enumerate((13, 15)):
         @pl.when(core == q)
@@ -429,7 +436,7 @@
         dma = pltpu.SemaphoreType.DMA
         outs = [
             vmem(z_rows.shape, BF16), vmem((n_seq, n_loc * hid), BF16), vmem((8 * LANES, 4 * pair), BF16),
-            vmem((2, 2 * BLOCK, 4 * pair), F32), vmem((2, 2, BLOCK // 2, n_seq // 2), BF16),
+            vmem((2, 2 * BLOCK, 4 * pair), F32), vmem((2, 2, BLOCK // 4, n_seq // 2), BF16),
         ]
         vmem_spec = pl.BlockSpec(memory_space=pltpu.VMEM)
         made = pl.pallas_call(

time: 43.6 us -> 43.4 us (level)
  no operation moved by 1% of the time
where the time goes in v7:
time: 43.4 us; the launch traced here: 43.3 us
  Pallas kernels  43.1 us (99%)
    pallas_call x1, Pallas kernels, local_update(): pl.pallas_call(functools.partial(kernel, n_dev), out_shape=outs, in_specs...  41.7 us
    pallas_call x1, Pallas kernels, local_update(): pl.pallas_call(functools.partial(last_kernel, n_dev), out_shape=jax.Shape...  1.41 us

profile of v7, /device:TPU:81, one launch (start us, length us, event | category | flops | bytes accessed | tf_op | source)
XLA Modules:
  0.0 43.3 jit_solution(13556059324262543966)
XLA Ops:
  0.0 41.7 %outer_mean_ring.1 = (bf16[32,256,128]{2,1,0:T(8,128)(2,1)S(1)}, bf16[512,1024]{1,0:T(8,128)(2,1)S(1)}, bf16[1024,512]{1,0:T(8,128)(2,1)S(1)}, f32[2,256,512]{2,1,0:T(8,128)S(1)}, bf16[2,2,32,256]{3,2,1,0:T(8,128)(2,1)S(1)}) custom-call(bf16[32,256,128]{2,1,0:T(8,128)(2,1)} %z_hbm.1, bf16[2048,512]{1,0:T(8,128)(2,1)} %bitcast.5, bf16[64]{0:T(256)(128)(2,1)} %ls_hbm.1, ...), custom_call_target="tpu_custom_call" | custom-call | tf_op jit(solution)/shard_map/outer_mean_ring/pallas_call | solution.py:442
  41.7 1.4 %outer_mean_last.1 = bf16[32,256,128]{2,1,0:T(8,128)(2,1)} custom-call(bf16[32,256,128]{2,1,0:T(8,128)(2,1)S(1)} %get-tuple-element.10.z_buf, bf16[512,1024]{1,0:T(8,128)(2,1)S(1)} %get-tuple-element.11.a_mat, bf16[1024,512]{1,0:T(8,128)(2,1)S(1)} %get-tuple-element.12.w_last, f32[2,256,512]{2,1,0:T(8,128)S(1)} %get-tuple-element.13.u_last, ...), custom_call_target="tpu_custom_call" | custom-call | tf_op jit(solution)/shard_map/outer_mean_last/pallas_call | solution.py:465
